TPU v7x, 256 devices: a 4x2x16 block of a 4x16x16 slice. The times are simulated.
256 devices in a mesh: groups: 2 (over y), nodes: 128 (over z, x, core).
Axes of the slice: x: 4, y: 2, z: 16, core: 2. Of those that a mesh axis runs over, the one named last changes fastest.
The devices are a block of a 4x16x16 slice.
Arguments:
- grid_latents: bfloat16 [262144, 1024], P(('groups', 'nodes')), parts along dimension 0, may hold values from -16 to 16
- mesh_latents: bfloat16 [65536, 1024], P(('groups', 'nodes')), parts along dimension 0, may hold values from -16 to 16
- neighbour_tiles: int32 [256, 6], P('nodes'), may hold values from 0 to 1023, as said below
- neighbour_live: int32 [256, 6], P('nodes'), may hold values from 0 to 1, as said below
- w_query: bfloat16 [1024, 1024], replicated, may hold values from -0.1875 to 0.1875
- w_keyval: bfloat16 [1024, 2048], replicated, may hold values from -0.1875 to 0.1875
- w_out: bfloat16 [1024, 1024], replicated, may hold values from -0.375 to 0.375
Outputs:
- mesh_next: float32 [65536, 1024], P(('groups', 'nodes')), parts along dimension 0
There are 2 independent parts, one for each index of `groups`. A program takes and returns all parts, laid end to end along the dimension named above; an argument that names none is the same for every part. Nothing has to cross between parts.
Inputs may be any that keep to these rules, and one draw needn't show every extreme that they name: `neighbour_tiles`: tile t lies on device t // 8 along nodes and mesh tile m on device m // 2; every listed tile lies on a device at most 2 indices away cyclically. The 6 entries of one mesh tile are distinct. Among the live entries of one device's mesh tiles at most 2 distinct tiles come from any one other device, and on every device some other device gives exactly 2. `neighbour_live`: each mesh tile has 2 to 6 live entries.
All inputs are finite; a program needn't handle non-finite values.
Results may differ from a plain program's by a relative error of at most 0.002.
The roundings to bfloat16 on the way count: a program that leaves them out, or rounds other values in their place, can miss the bound.
Values may be sent and summed in bfloat16 or wider, within the bound.
No kernel may reach another device: no remote copies, remote signals or barrier semaphores. Data moves between devices by JAX's collectives and lax.ppermute only.
A program may use at most 128 MiB of HBM per device.

v0:
```python
import jax
import jax.numpy as jnp
from jax import lax
from jax.sharding import PartitionSpec as P

HEADS = 16
TILE = 128
REACH = 2


def from_behind(block, axis, distance):
    devices = range(lax.axis_size(axis))
    route = [((i - distance) % len(devices), i) for i in devices]
    return lax.ppermute(block, axis, route)


def fetch(block, offset):
    return from_behind(block, "nodes", -offset)


def pick_tile(sources, source_index, local_index):
    picked = lax.dynamic_index_in_dim(sources[0], local_index, 0, keepdims=False)
    for number in range(1, len(sources)):
        other = lax.dynamic_index_in_dim(sources[number], local_index, 0, keepdims=False)
        picked = jnp.where(source_index == number, other, picked)
    return picked


def attend_one(query_tile, slot_tiles, live_row):
    tile_rows, model_width = query_tile.shape
    head_size = model_width // HEADS
    query_heads = query_tile.reshape(tile_rows, HEADS, head_size)
    score_blocks = []
    value_blocks = []
    for slot, tile in enumerate(slot_tiles):
        key_heads = tile[:, :model_width].reshape(tile_rows, HEADS, head_size)
        value_blocks.append(tile[:, model_width:].reshape(tile_rows, HEADS, head_size))
        block = jnp.einsum(
            "qhd,khd->hqk", query_heads, key_heads, preferred_element_type=jnp.float32
        )
        block = block * head_size ** (-0.5)
        score_blocks.append(jnp.where(live_row[slot] > 0, block, -1e30))
    scores = jnp.concatenate(score_blocks, axis=-1)
    row_top = jnp.max(scores, axis=-1, keepdims=True)
    raised = jnp.exp(scores - row_top)
    row_total = jnp.sum(raised, axis=-1, keepdims=True)
    weights = (raised / row_total).astype(jnp.bfloat16)
    mixture = jnp.zeros((tile_rows, HEADS, head_size), jnp.float32)
    for slot, values in enumerate(value_blocks):
        part_weights = weights[:, :, slot * tile_rows : (slot + 1) * tile_rows]
        mixture = mixture + jnp.einsum(
            "hqk,khd->qhd", part_weights, values, preferred_element_type=jnp.float32
        )
    return mixture.astype(jnp.bfloat16).reshape(tile_rows, model_width)


def per_device(
    grid_latents, mesh_latents, neighbour_tiles, neighbour_live, w_query, w_keyval, w_out
):
    model_width = w_query.shape[0]
    tile_rows = TILE
    own_tiles = grid_latents.shape[0] // tile_rows
    mesh_tiles = mesh_latents.shape[0] // tile_rows
    node_count = lax.axis_size("nodes")
    position = lax.axis_index("nodes")
    offsets = [shift_by for shift_by in range(-REACH, REACH + 1) if shift_by != 0]
    payload = grid_latents.reshape(own_tiles, tile_rows, model_width)
    tile_owner = neighbour_tiles // own_tiles
    tile_local = neighbour_tiles % own_tiles
    tile_offset = (tile_owner - position + node_count + REACH) % node_count - REACH
    source_index = jnp.zeros(neighbour_tiles.shape, jnp.int32)
    local_index = jnp.where(tile_offset == 0, tile_local, 0)
    received = []
    for offset_index, offset in enumerate(offsets):
        received.append(fetch(payload, offset))
        source_index = jnp.where(tile_offset == offset, offset_index + 1, source_index)
        local_index = jnp.where(tile_offset == offset, tile_local, local_index)
    sources = [payload] + received
    projected = []
    for source in sources:
        depth = source.shape[0]
        flat = jnp.dot(
            source.reshape(depth * tile_rows, model_width),
            w_keyval,
            preferred_element_type=jnp.float32,
        )
        projected.append(flat.astype(jnp.bfloat16).reshape(depth, tile_rows, 2 * model_width))
    sources = projected
    queries = jnp.dot(mesh_latents, w_query, preferred_element_type=jnp.float32).astype(
        jnp.bfloat16
    )
    queries = queries.reshape(mesh_tiles, tile_rows, model_width)
    outputs = []
    for mesh_tile in range(mesh_tiles):
        slot_tiles = [
            pick_tile(sources, source_index[mesh_tile, slot], local_index[mesh_tile, slot])
            for slot in range(neighbour_tiles.shape[1])
        ]
        outputs.append(attend_one(queries[mesh_tile], slot_tiles, neighbour_live[mesh_tile]))
    attended = jnp.concatenate(outputs, axis=0)
    return mesh_latents.astype(jnp.float32) + jnp.dot(
        attended, w_out, preferred_element_type=jnp.float32
    )


def solution(mesh):
    return jax.shard_map(
        per_device,
        mesh=mesh,
        in_specs=(
            P(("groups", "nodes"), None),
            P(("groups", "nodes"), None),
            P("nodes", None),
            P("nodes", None),
            P(),
            P(),
            P(),
        ),
        out_specs=P(("groups", "nodes"), None),
        check_vma=False,
    )
```

profile of v0, /device:TPU:40, one launch (start us, length us, event | category | flops | bytes accessed | tf_op | source)
XLA Modules:
  0.0 189.4 jit_solution(9329232743319636379)
XLA Ops:
  0.0 1.6 collective-permute-start.3
  1.6 23.1 %collective-permute-start.1 = (bf16[8,128,1024]{2,1,0:T(8,128)(2,1)}, bf16[8,128,1024]{2,1,0:T(8,128)(2,1)}, u32[]{:S(2)}, u32[]{:S(2)}) collective-permute-start(bf16[8,128,1024]{2,1,0:T(8,128)(2,1)} %bitcast.257), channel_id=1, source_target_pairs={{1,0},{2,1},{3,2},{4,3},{5,4},{6,5},{7,6},{8,7},{9,8},{10,9},{11,1... | collective-permute-start | bytes 6291464 | tf_op jit(solution)/shard_map/ppermute | solution.py:14
  24.8 2.1 %collective-permute-start = (bf16[8,128,1024]{2,1,0:T(8,128)(2,1)}, bf16[8,128,1024]{2,1,0:T(8,128)(2,1)}, u32[]{:S(2)}, u32[]{:S(2)}) collective-permute-start(bf16[8,128,1024]{2,1,0:T(8,128)(2,1)} %bitcast.258), channel_id=1, source_target_pairs={{2,0},{3,1},{4,2},{5,3},{6,4},{7,5},{8,6},{9,7},{10,8},{11,9},{12,... | collective-permute-start | bytes 6291464 | tf_op jit(solution)/shard_map/ppermute | solution.py:14
  74.4 1.8 fusion.66
  83.6 1.8 convolution_convert_fusion.5
  85.3 9.3 %convolution_convert_fusion = bf16[1024,2048]{1,0:T(8,128)(2,1)} fusion(bf16[1024,1024]{1,0:T(8,128)(2,1)} %param.7, bf16[1024,2048]{1,0:T(8,128)(2,1)} %param.12), kind=kOutput, calls=%fused_computation.6 | convolution fusion | flops 4297064448 | bytes 10485760 | tf_op jit(solution)/shard_map/dot_general | solution.py:82
  103.9 7.5 %convolution_convert_fusion.1 = bf16[1024,2048]{1,0:T(8,128)(2,1)S(1)} fusion(bf16[1024,1024]{1,0:T(8,128)(2,1)} %bitcast.12, bf16[1024,2048]{1,0:T(8,128)(2,1)} %param.12), kind=kOutput, calls=%fused_computation.7 | convolution fusion | flops 4297064448 | bytes 10485760 | tf_op jit(solution)/shard_map/dot_general | solution.py:82
  111.4 7.8 %convolution_convert_fusion.2 = bf16[1024,2048]{1,0:T(8,128)(2,1)S(1)} fusion(bf16[1024,1024]{1,0:T(8,128)(2,1)} %bitcast.9, bf16[1024,2048]{1,0:T(8,128)(2,1)S(1)} %copy-done.22), kind=kOutput, calls=%fused_computation.8 | convolution fusion | flops 4297064448 | bytes 10485760 | tf_op jit(solution)/shard_map/dot_general | solution.py:82
  119.2 7.8 %convolution_convert_fusion.3 = bf16[1024,2048]{1,0:T(8,128)(2,1)S(1)} fusion(bf16[1024,1024]{1,0:T(8,128)(2,1)} %bitcast.6, bf16[1024,2048]{1,0:T(8,128)(2,1)S(1)} %copy-done.22), kind=kOutput, calls=%fused_computation.9 | convolution fusion | flops 4297064448 | bytes 10485760 | tf_op jit(solution)/shard_map/dot_general | solution.py:82
  127.1 7.8 %convolution_convert_fusion.4 = bf16[1024,2048]{1,0:T(8,128)(2,1)S(1)} fusion(bf16[1024,1024]{1,0:T(8,128)(2,1)} %bitcast.2, bf16[1024,2048]{1,0:T(8,128)(2,1)S(1)} %copy-done.22), kind=kOutput, calls=%fused_computation.10 | convolution fusion | flops 4297064448 | bytes 10485760 | tf_op jit(solution)/shard_map/dot_general | solution.py:82
  135.0 2.4 %select_bitcast_fusion.6 = (bf16[128,2048]{1,0:T(8,128)(2,1)S(1)}, bf16[128,2048]{1,0:T(8,128)(2,1)S(1)}) fusion(bf16[8,128,2048]{2,1,0:T(8,128)(2,1)} %bitcast.187, s32[]{:T(128)S(6)} %select_n.640, bf16[8,128,2048]{2,1,0:T(8,128)(2,1)S(1)} %bitcast.193, bf16[8,128,2048]{2,1,0:T(8,128)(2,1)S(1)} %bitcast.199, bf16[8,128,2048]{2,1,0:T(8,128)(2,1)S(1)} %bitcast.205, ...), kind=kLoop, calls=%fused_computation.72 | loop fusion | flops 2097152 | bytes 6291472 | tf_op jit(solution)/shard_map/jit(_where)/select_n | solution.py:25
  140.9 2.7 %select_bitcast_fusion.7 = (bf16[128,2048]{1,0:T(8,128)(2,1)S(1)}, bf16[128,2048]{1,0:T(8,128)(2,1)S(1)}) fusion(bf16[8,128,2048]{2,1,0:T(8,128)(2,1)} %bitcast.188, s32[]{:T(128)S(6)} %select_n.628, bf16[8,128,2048]{2,1,0:T(8,128)(2,1)} %bitcast.194, bf16[8,128,2048]{2,1,0:T(8,128)(2,1)} %bitcast.200, bf16[8,128,2048]{2,1,0:T(8,128)(2,1)} %bitcast.206, ...), kind=kLoop, calls=%fused_computation.73 | loop fusion | flops 2097152 | bytes 6291472 | tf_op jit(solution)/shard_map/jit(_where)/select_n | solution.py:25
  145.7 2.7 %select_bitcast_fusion.8 = (bf16[128,2048]{1,0:T(8,128)(2,1)S(1)}, bf16[128,2048]{1,0:T(8,128)(2,1)S(1)}) fusion(bf16[8,128,2048]{2,1,0:T(8,128)(2,1)} %bitcast.189, s32[]{:T(128)S(6)} %select_n.616, bf16[8,128,2048]{2,1,0:T(8,128)(2,1)} %bitcast.195, bf16[8,128,2048]{2,1,0:T(8,128)(2,1)} %bitcast.201, bf16[8,128,2048]{2,1,0:T(8,128)(2,1)} %bitcast.207, ...), kind=kLoop, calls=%fused_computation.74 | loop fusion | flops 2097152 | bytes 6291472 | tf_op jit(solution)/shard_map/jit(_where)/select_n | solution.py:25
  150.6 2.7 %select_bitcast_fusion.9 = (bf16[128,2048]{1,0:T(8,128)(2,1)S(1)}, bf16[128,2048]{1,0:T(8,128)(2,1)S(1)}) fusion(bf16[8,128,2048]{2,1,0:T(8,128)(2,1)} %bitcast.190, s32[]{:T(128)S(6)} %select_n.604, bf16[8,128,2048]{2,1,0:T(8,128)(2,1)} %bitcast.196, bf16[8,128,2048]{2,1,0:T(8,128)(2,1)} %bitcast.202, bf16[8,128,2048]{2,1,0:T(8,128)(2,1)} %bitcast.208, ...), kind=kLoop, calls=%fused_computation.75 | loop fusion | flops 2097152 | bytes 6291472 | tf_op jit(solution)/shard_map/jit(_where)/select_n | solution.py:25
  155.4 2.7 %select_bitcast_fusion.10 = (bf16[128,2048]{1,0:T(8,128)(2,1)S(1)}, bf16[128,2048]{1,0:T(8,128)(2,1)S(1)}) fusion(bf16[8,128,2048]{2,1,0:T(8,128)(2,1)} %bitcast.191, s32[]{:T(128)S(6)} %select_n.592, bf16[8,128,2048]{2,1,0:T(8,128)(2,1)} %bitcast.197, bf16[8,128,2048]{2,1,0:T(8,128)(2,1)} %bitcast.203, bf16[8,128,2048]{2,1,0:T(8,128)(2,1)} %bitcast.209, ...), kind=kLoop, calls=%fused_computation.76 | loop fusion | flops 2097152 | bytes 6291472 | tf_op jit(solution)/shard_map/jit(_where)/select_n | solution.py:25
  159.2 2.7 %select_bitcast_fusion.11 = (bf16[128,2048]{1,0:T(8,128)(2,1)S(1)}, bf16[128,2048]{1,0:T(8,128)(2,1)S(1)}) fusion(bf16[8,128,2048]{2,1,0:T(8,128)(2,1)} %bitcast.192, s32[]{:T(128)S(6)} %select_n.579, bf16[8,128,2048]{2,1,0:T(8,128)(2,1)} %bitcast.198, bf16[8,128,2048]{2,1,0:T(8,128)(2,1)} %bitcast.204, bf16[8,128,2048]{2,1,0:T(8,128)(2,1)} %bitcast.210, ...), kind=kLoop, calls=%fused_computation.77 | loop fusion | flops 2097152 | bytes 6291472 | tf_op jit(solution)/shard_map/jit(_where)/select_n | solution.py:25
  164.9 1.8 copy.77
  166.7 1.8 copy.59
  168.6 1.8 copy.78
  170.4 1.8 copy.84
  172.2 1.4 fusion.48
  173.6 1.4 fusion.47
  175.1 1.3 fusion.49
  187.7 1.7 convolution_add_fusion
  (111 shorter events, 29.5 us)
Async XLA Ops:
  0.0 83.6 %copy-start = (bf16[1024,1024]{1,0:T(8,128)(2,1)S(1)}, bf16[1024,1024]{1,0:T(8,128)(2,1)}, u32[]{:S(2)}) copy-start(bf16[1024,1024]{1,0:T(8,128)(2,1)} %param.11) | copy-start | bytes 6291460
  0.0 103.9 %collective-permute-start.3 = (bf16[8,128,1024]{2,1,0:T(8,128)(2,1)}, bf16[8,128,1024]{2,1,0:T(8,128)(2,1)}, u32[]{:S(2)}, u32[]{:S(2)}) collective-permute-start(bf16[8,128,1024]{2,1,0:T(8,128)(2,1)} %bitcast.255), channel_id=1, source_target_pairs={{126,0},{127,1},{0,2},{1,3},{2,4},{3,5},{4,6},{5,7},{6,8},{7,9},{8... | collective-permute-start | bytes 6291464 | tf_op jit(solution)/shard_map/ppermute | solution.py:14
  1.6 109.7 %collective-permute-start.2 = (bf16[8,128,1024]{2,1,0:T(8,128)(2,1)}, bf16[8,128,1024]{2,1,0:T(8,128)(2,1)}, u32[]{:S(2)}, u32[]{:S(2)}) collective-permute-start(bf16[8,128,1024]{2,1,0:T(8,128)(2,1)} %bitcast.256), channel_id=1, source_target_pairs={{127,0},{0,1},{1,2},{2,3},{3,4},{4,5},{5,6},{6,7},{7,8},{8,9},{9,1... | collective-permute-start | bytes 6291464 | tf_op jit(solution)/shard_map/ppermute | solution.py:14
  1.6 117.6 %collective-permute-start.1 = (bf16[8,128,1024]{2,1,0:T(8,128)(2,1)}, bf16[8,128,1024]{2,1,0:T(8,128)(2,1)}, u32[]{:S(2)}, u32[]{:S(2)}) collective-permute-start(bf16[8,128,1024]{2,1,0:T(8,128)(2,1)} %bitcast.257), channel_id=1, source_target_pairs={{1,0},{2,1},{3,2},{4,3},{5,4},{6,5},{7,6},{8,7},{9,8},{10,9},{11,1... | collective-permute-start | bytes 6291464 | tf_op jit(solution)/shard_map/ppermute | solution.py:14
  24.8 102.3 %collective-permute-start = (bf16[8,128,1024]{2,1,0:T(8,128)(2,1)}, bf16[8,128,1024]{2,1,0:T(8,128)(2,1)}, u32[]{:S(2)}, u32[]{:S(2)}) collective-permute-start(bf16[8,128,1024]{2,1,0:T(8,128)(2,1)} %bitcast.258), channel_id=1, source_target_pairs={{2,0},{3,1},{4,2},{5,3},{6,4},{7,5},{8,6},{9,7},{10,8},{11,9},{12,... | collective-permute-start | bytes 6291464 | tf_op jit(solution)/shard_map/ppermute | solution.py:14
  103.9 7.5 %copy-start.22 = (bf16[1024,2048]{1,0:T(8,128)(2,1)S(1)}, bf16[1024,2048]{1,0:T(8,128)(2,1)}, u32[]{:S(2)}) copy-start(bf16[1024,2048]{1,0:T(8,128)(2,1)} %param.12) | copy-start | bytes 12582916
  111.3 23.6 %copy-start.2 = (bf16[1024,2048]{1,0:T(8,128)(2,1)}, bf16[1024,2048]{1,0:T(8,128)(2,1)S(1)}, u32[]{:S(2)}) copy-start(bf16[1024,2048]{1,0:T(8,128)(2,1)S(1)} %convolution_convert_fusion.1) | copy-start | bytes 12582916
  119.2 15.8 %copy-start.3 = (bf16[1024,2048]{1,0:T(8,128)(2,1)}, bf16[1024,2048]{1,0:T(8,128)(2,1)S(1)}, u32[]{:S(2)}) copy-start(bf16[1024,2048]{1,0:T(8,128)(2,1)S(1)} %convolution_convert_fusion.2) | copy-start | bytes 12582916
  127.1 7.9 %copy-start.4 = (bf16[1024,2048]{1,0:T(8,128)(2,1)}, bf16[1024,2048]{1,0:T(8,128)(2,1)S(1)}, u32[]{:S(2)}) copy-start(bf16[1024,2048]{1,0:T(8,128)(2,1)S(1)} %convolution_convert_fusion.3) | copy-start | bytes 12582916
  134.9 2.5 %copy-start.5 = (bf16[1024,2048]{1,0:T(8,128)(2,1)}, bf16[1024,2048]{1,0:T(8,128)(2,1)S(1)}, u32[]{:S(2)}) copy-start(bf16[1024,2048]{1,0:T(8,128)(2,1)S(1)} %convolution_convert_fusion.4) | copy-start | bytes 12582916
  162.8 12.2 %copy-start.12 = (bf16[128,1024]{0,1:T(8,128)(2,1)S(1)}, bf16[128,1024]{0,1:T(8,128)(2,1)}, u32[]{:S(2)}) copy-start(bf16[128,1024]{0,1:T(8,128)(2,1)} %copy.76) | copy-start | bytes 786436
  163.6 12.7 %copy-start.19 = (bf16[128,1024]{0,1:T(8,128)(2,1)S(1)}, bf16[128,1024]{0,1:T(8,128)(2,1)}, u32[]{:S(2)}) copy-start(bf16[128,1024]{0,1:T(8,128)(2,1)} %copy.80) | copy-start | bytes 786436
  166.7 10.0 %copy-start.17 = (bf16[128,1024]{0,1:T(8,128)(2,1)S(1)}, bf16[128,1024]{0,1:T(8,128)(2,1)}, u32[]{:S(2)}) copy-start(bf16[128,1024]{0,1:T(8,128)(2,1)} %copy.81) | copy-start | bytes 786436
  172.2 5.0 %copy-start.15 = (bf16[128,1024]{0,1:T(8,128)(2,1)S(1)}, bf16[128,1024]{0,1:T(8,128)(2,1)}, u32[]{:S(2)}) copy-start(bf16[128,1024]{0,1:T(8,128)(2,1)} %copy.82) | copy-start | bytes 786436
  178.4 1.5 copy-start.21
  178.4 1.9 copy-start.18
  179.5 1.6 copy-start.14
  179.5 1.9 %copy-start.13 = (bf16[128,1024]{0,1:T(8,128)(2,1)S(1)}, bf16[128,1024]{0,1:T(8,128)(2,1)}, u32[]{:S(2)}) copy-start(bf16[128,1024]{0,1:T(8,128)(2,1)} %copy.63) | copy-start | bytes 786436
  182.7 1.6 copy-start.7
  184.0 1.4 copy-start.9
  185.7 1.4 copy-start.8
  186.0 1.6 copy-start.6
  186.0 1.7 copy-start.10
  186.5 2.8 %copy-start.1 = (bf16[1024,1024]{1,0:T(8,128)(2,1)S(1)}, bf16[1024,1024]{1,0:T(8,128)(2,1)}, u32[]{:S(2)}) copy-start(bf16[1024,1024]{1,0:T(8,128)(2,1)} %param.11) | copy-start | bytes 6291460
  (3 other events, 3.4 us)
where the time goes:
time: 191 us; the launch traced here: 189 us
  between operations  60.3 us (32%)
  matrix products  54.4 us (28%)
  starting transfers between devices  26.8 us (14%)
  local copies, waits for them, and re-layouts  26.5 us (14%)
  other arithmetic  21.3 us (11%)
    dot_general x5, matrix products, per_device(): jnp.dot(source.reshape(depth * tile_rows, model_width), w_keyval, preferr...  40.2 us
    ppermute x4, starting transfers between devices, from_behind(): return lax.ppermute(block, axis, route)  26.8 us
    select_n x6, other arithmetic, pick_tile(): picked = jnp.where(source_index == number, other, picked)  15.9 us
    slice x13, local copies, waits for them, and re-layouts, attend_one(): key_heads = tile[:, :model_width].reshape(tile_rows, HEADS, head_size)  14 us
    dot_general x12, matrix products, attend_one(): jnp.einsum('qhd,khd->hqk', query_heads, key_heads, preferred_element_type...  7.44 us
    slice x17, local copies, waits for them, and re-layouts, attend_one(): tile[:, model_width:].reshape(tile_rows, HEADS, head_size)  7.21 us
  transfers between devices with their start and end apart: 4, of which 0 were waited for; matrix products, arithmetic and copies ran while one was open for 21% of the time, Pallas kernels for 0%

commit v1 on v0

v1 whole, which is shorter than its diff:
```python
import functools

import jax
import jax.numpy as jnp
from jax import lax
from jax.experimental import pallas as pl
from jax.experimental.pallas import tpu as pltpu
from jax.sharding import PartitionSpec as P


HEADS = 16
TILE = 128
REACH = 2
CAP = 2
LOW = -1e30

SMEM = pl.BlockSpec(memory_space=pltpu.SMEM)
VMEM = pl.BlockSpec(memory_space=pltpu.VMEM)
HBM = pl.BlockSpec(memory_space=pltpu.HBM)
MIB = 1 << 20


def partner_of(i, n):
    return i + 1 - 2 * (i % 2)


def cross_of(i, n):
    return (i + n - 1 + 2 * (i % 2)) % n


def ahead_of(i, n):
    return (i + REACH) % n


def behind_of(i, n):
    return (i + n - REACH) % n


SOURCES = (behind_of, ahead_of, cross_of, partner_of)
STAGES = ((3,), (0, 1))
LAST = 2


def span_of(listed, base, own):
    low = jnp.int32(own)
    high = jnp.int32(-1)
    for entry in listed:
        local = entry - base
        held = (local >= 0) & (local < own)
        low = jnp.minimum(low, jnp.where(held, local, own))
        high = jnp.maximum(high, jnp.where(held, local, -1))
    return low, high


def entries(ref):
    return [ref[i, j] for i in range(ref.shape[0]) for j in range(ref.shape[1])]


def pack_kernel(*refs):
    count = len(SOURCES)
    asked, grid, outs = refs[:count], refs[count], refs[count + 1 :]
    own = grid.shape[0]
    me = lax.axis_index("nodes")
    for c in range(count):
        low, high = span_of(entries(asked[c]), me * own, own)
        low = jnp.where(high < 0, 0, low)
        high = jnp.maximum(high, 0)
        outs[c][0] = grid[low]
        outs[c][1] = grid[high]


def pack(asked, grid):
    count = len(SOURCES)
    shape = jax.ShapeDtypeStruct((CAP,) + grid.shape[1:], grid.dtype)
    return pl.pallas_call(
        pack_kernel,
        out_shape=[shape] * count,
        in_specs=[SMEM] * count + [VMEM],
        out_specs=[VMEM] * count,
        compiler_params=pltpu.CompilerParams(vmem_limit_bytes=4 * MIB),
        name="pack",
    )(*asked, grid)


def project(rows_ref, w_keyval, keys, values, model_width):
    rows = rows_ref.shape[0]
    step = 256
    depth = min(rows, 512)
    for at in range(0, rows, depth):
        block = rows_ref[at : at + depth, :]
        for column in range(0, model_width, step):
            part = jnp.dot(
                block, w_keyval[:, column : column + step], preferred_element_type=jnp.float32
            )
            keys[at : at + depth, column : column + step] = part.astype(jnp.bfloat16)
            part = jnp.dot(
                block,
                w_keyval[:, model_width + column : model_width + column + step],
                preferred_element_type=jnp.float32,
            )
            turned = part.astype(jnp.bfloat16).T
            for k in range(depth // TILE):
                values[at // TILE + k, column : column + step, :] = turned[
                    :, k * TILE : (k + 1) * TILE
                ]


def add_tile(tile, mesh_tile, keys, values, queries, tops, totals, mixed):
    pairs = queries.shape[1]
    width = queries.shape[2]
    head = width // 2
    start = pl.multiple_of(tile * TILE, TILE)
    for pair in range(pairs):
        lanes = slice(pair * width, (pair + 1) * width)
        scores = jnp.dot(
            keys[pl.ds(start, TILE), lanes],
            queries[mesh_tile, pair],
            preferred_element_type=jnp.float32,
        )
        old = tops[mesh_tile, pair : pair + 1, :]
        new = jnp.maximum(old, jnp.max(scores, axis=0, keepdims=True))
        shrink = jnp.exp(old - new)
        raised = jnp.exp(scores - new)
        tops[mesh_tile, pair : pair + 1, :] = new
        totals[mesh_tile, pair : pair + 1, :] = totals[
            mesh_tile, pair : pair + 1, :
        ] * shrink + jnp.sum(raised, axis=0, keepdims=True)
        weights = raised.astype(jnp.bfloat16)
        for k in range(2):
            rows = slice(pair * width + k * head, pair * width + (k + 1) * head)
            cols = slice(k * TILE, (k + 1) * TILE)
            part = jnp.dot(
                values[tile, rows, :], weights[:, cols], preferred_element_type=jnp.float32
            )
            mixed[mesh_tile, rows, :] = mixed[mesh_tile, rows, :] * shrink[:, cols] + part


def lists(tiles_ref, live_ref, mesh_tile, wanted):
    found = jnp.bool_(False)
    for j in range(tiles_ref.shape[1]):
        found = found | ((live_ref[mesh_tile, j] > 0) & (tiles_ref[mesh_tile, j] == wanted))
    return found


def add_listed(count, keep, tiles_ref, live_ref, *state):
    mesh_tiles = tiles_ref.shape[0]

    def body(i, carry):
        tile = i // mesh_tiles
        mesh_tile = i % mesh_tiles
        wanted, fresh = keep(tile)

        @pl.when(fresh & lists(tiles_ref, live_ref, mesh_tile, wanted))
        def _():
            add_tile(tile, mesh_tile, *state)

        return carry

    lax.fori_loop(0, count * mesh_tiles, body, 0)


def front_kernel(mesh_hbm, w_query_hbm, grid_hbm, w_keyval_hbm, queries, grid, w_keyval, mesh, w_query, sems):
    model_width = w_query.shape[0]
    width = queries.shape[2]
    head = width // 2
    step = 256
    copies = [
        pltpu.make_async_copy(source, target, sems.at[k])
        for k, (source, target) in enumerate(
            (
                (mesh_hbm, mesh),
                (w_query_hbm, w_query),
                (grid_hbm, grid),
                (w_keyval_hbm, w_keyval),
            )
        )
    ]
    for copy in copies:
        copy.start()
    queries[...] = jnp.zeros(queries.shape, queries.dtype)
    copies[0].wait()
    copies[1].wait()
    for column in range(0, model_width, step):
        part = jnp.dot(
            mesh[...], w_query[:, column : column + step], preferred_element_type=jnp.float32
        )
        turned = (part.astype(jnp.bfloat16) * jnp.bfloat16(head ** -0.5)).T
        for m in range(queries.shape[0]):
            for h in range(step // head):
                which = column // head + h
                k = which % 2
                queries[m, which // 2, k * head : (k + 1) * head, k * TILE : (k + 1) * TILE] = turned[
                    h * head : (h + 1) * head, m * TILE : (m + 1) * TILE
                ]
    copies[2].wait()
    copies[3].wait()


def own_kernel(tiles_ref, live_ref, grid, w_keyval, queries, tops, totals, mixed, keys, values):
    own = grid.shape[0] // TILE
    tops[...] = jnp.full(tops.shape, LOW, jnp.float32)
    totals[...] = jnp.zeros(totals.shape, jnp.float32)
    mixed[...] = jnp.zeros(mixed.shape, jnp.float32)
    project(grid, w_keyval, keys, values, w_keyval.shape[0])
    base = lax.axis_index("nodes") * own

    def keep(tile):
        return base + tile, jnp.bool_(True)

    add_listed(own, keep, tiles_ref, live_ref, keys, values, queries, tops, totals, mixed)


def chunk_update(sources, own, tiles_ref, live_ref, rows_ref, w_keyval, keys, values, *state):
    me = lax.axis_index("nodes")
    n = lax.axis_size("nodes")
    listed = [
        jnp.where(live > 0, tile, -1)
        for tile, live in zip(entries(tiles_ref), entries(live_ref))
    ]
    project(rows_ref, w_keyval, keys, values, w_keyval.shape[0])
    wanted = []
    for source in sources:
        base = source(me, n) * own
        low, high = span_of(listed, base, own)
        wanted.append(jnp.where(low < own, base + low, -1))
        wanted.append(jnp.where(low < high, base + high, -1))

    def keep(tile):
        found = wanted[0]
        for k in range(1, len(wanted)):
            found = jnp.where(tile == k, wanted[k], found)
        return found, found >= 0

    add_listed(len(wanted), keep, tiles_ref, live_ref, keys, values, *state)


def chunk_kernel(sources, own, tiles_ref, live_ref, w_keyval, queries, tops_in, totals_in, mixed_in, *refs):
    count = len(sources)
    chunks, (tops, totals, mixed, rows, keys, values) = refs[:count], refs[count:]
    tops[...] = tops_in[...]
    totals[...] = totals_in[...]
    mixed[...] = mixed_in[...]
    for k, chunk in enumerate(chunks):
        size = chunk.shape[0]
        rows[k * size : (k + 1) * size, :] = chunk[...]
    chunk_update(sources, own, tiles_ref, live_ref, rows, w_keyval, keys, values, queries, tops, totals, mixed)


def last_kernel(sources, own, tiles_ref, live_ref, w_keyval, queries, tops_in, totals_in, mixed_in, chunk, mesh, w_out, out, tops, totals, mixed, keys, values):
    tops[...] = tops_in[...]
    totals[...] = totals_in[...]
    mixed[...] = mixed_in[...]
    chunk_update(sources, own, tiles_ref, live_ref, chunk, w_keyval, keys, values, queries, tops, totals, mixed)
    pairs = queries.shape[1]
    width = queries.shape[2]
    head = width // 2
    for m in range(queries.shape[0]):
        parts = []
        for pair in range(pairs):
            share = 1.0 / totals[m, pair : pair + 1, :]
            for k in range(2):
                rows = slice(pair * width + k * head, pair * width + (k + 1) * head)
                parts.append(
                    (mixed[m, rows, :] * share[:, k * TILE : (k + 1) * TILE]).astype(jnp.bfloat16)
                )
        attended = jnp.concatenate(parts, axis=0).T
        rows = slice(m * TILE, (m + 1) * TILE)
        out[rows, :] = mesh[rows, :].astype(jnp.float32) + jnp.dot(
            attended, w_out[...], preferred_element_type=jnp.float32
        )


def per_device(
    grid_latents, mesh_latents, neighbour_tiles, neighbour_live, w_query, w_keyval, w_out
):
    model_width = w_query.shape[0]
    own = grid_latents.shape[0] // TILE
    mesh_tiles = mesh_latents.shape[0] // TILE
    n = lax.axis_size("nodes")
    pairs = HEADS // 2
    width = model_width // pairs

    def to_sources(block, source):
        return lax.ppermute(block, "nodes", [(i, source(i, n)) for i in range(n)])

    def from_sources(block, source):
        return lax.ppermute(block, "nodes", [(source(i, n), i) for i in range(n)])

    f32 = jnp.float32
    bf16 = jnp.bfloat16
    stat = jax.ShapeDtypeStruct((mesh_tiles, pairs, 2 * TILE), f32)
    mix = jax.ShapeDtypeStruct((mesh_tiles, model_width, TILE), f32)
    query = jax.ShapeDtypeStruct((mesh_tiles, pairs, width, 2 * TILE), bf16)

    wanted = jnp.where(neighbour_live > 0, neighbour_tiles, -1)
    asked = []
    for source in SOURCES:
        asked.append(to_sources(wanted, source))
    stored = [
        pltpu.with_memory_space_constraint(array, pltpu.HBM)
        for array in (
            mesh_latents,
            w_query,
            grid_latents.reshape(own, TILE, model_width),
            w_keyval,
        )
    ]
    queries, grid, w_kv = pl.pallas_call(
        front_kernel,
        out_shape=[query, jax.ShapeDtypeStruct(stored[2].shape, bf16), jax.ShapeDtypeStruct(w_keyval.shape, bf16)],
        in_specs=[HBM] * 4,
        out_specs=[VMEM] * 3,
        scratch_shapes=[
            pltpu.VMEM(mesh_latents.shape, bf16),
            pltpu.VMEM(w_query.shape, bf16),
            pltpu.SemaphoreType.DMA((4,)),
        ],
        compiler_params=pltpu.CompilerParams(vmem_limit_bytes=8 * MIB),
        cost_estimate=pl.CostEstimate(flops=10**9, transcendentals=0, bytes_accessed=10**7),
        name="front",
    )(*stored)
    packed = pack(asked, grid)
    chunks = []
    for block, source in zip(packed, SOURCES):
        chunks.append(from_sources(block, source).reshape(CAP * TILE, model_width))
    tops, totals, mixed = pl.pallas_call(
        own_kernel,
        out_shape=[stat, stat, mix],
        in_specs=[SMEM, SMEM, VMEM, VMEM, VMEM],
        out_specs=[VMEM] * 3,
        scratch_shapes=[pltpu.VMEM((own * TILE, model_width), bf16), pltpu.VMEM((own, model_width, TILE), bf16)],
        compiler_params=pltpu.CompilerParams(vmem_limit_bytes=16 * MIB),
        cost_estimate=pl.CostEstimate(flops=6 * 10**9, transcendentals=0, bytes_accessed=10**7),
        name="own",
    )(neighbour_tiles, neighbour_live, grid.reshape(own * TILE, model_width), w_kv, queries)

    for members in STAGES:
        sources = [SOURCES[c] for c in members]
        rows = len(members) * CAP * TILE
        tops, totals, mixed = pl.pallas_call(
            functools.partial(chunk_kernel, sources, own),
            out_shape=[stat, stat, mix],
            in_specs=[SMEM, SMEM] + [VMEM] * (5 + len(members)),
            out_specs=[VMEM] * 3,
            scratch_shapes=[
                pltpu.VMEM((rows, model_width), bf16),
                pltpu.VMEM((rows, model_width), bf16),
                pltpu.VMEM((rows // TILE, model_width, TILE), bf16),
            ],
            input_output_aliases={4: 0, 5: 1, 6: 2},
            compiler_params=pltpu.CompilerParams(vmem_limit_bytes=12 * MIB),
            cost_estimate=pl.CostEstimate(flops=2 * 10**9, transcendentals=0, bytes_accessed=10**6),
            name="chunk",
        )(neighbour_tiles, neighbour_live, w_kv, queries, tops, totals, mixed, *[chunks[c] for c in members])
    return pl.pallas_call(
        functools.partial(last_kernel, [SOURCES[LAST]], own),
        out_shape=jax.ShapeDtypeStruct(mesh_latents.shape, f32),
        in_specs=[SMEM, SMEM] + [VMEM] * 8,
        out_specs=VMEM,
        scratch_shapes=[pltpu.VMEM(shape.shape, f32) for shape in (stat, stat, mix)]
        + [
            pltpu.VMEM((CAP * TILE, model_width), bf16),
            pltpu.VMEM((CAP, model_width, TILE), bf16),
        ],
        compiler_params=pltpu.CompilerParams(vmem_limit_bytes=12 * MIB),
        cost_estimate=pl.CostEstimate(flops=3 * 10**9, transcendentals=0, bytes_accessed=10**6),
        name="last",
    )(neighbour_tiles, neighbour_live, w_kv, queries, tops, totals, mixed, chunks[LAST], mesh_latents, w_out)


def solution(mesh):
    return jax.shard_map(
        per_device,
        mesh=mesh,
        in_specs=(
            P(("groups", "nodes"), None),
            P(("groups", "nodes"), None),
            P("nodes", None),
            P("nodes", None),
            P(),
            P(),
            P(),
        ),
        out_specs=P(("groups", "nodes"), None),
        check_vma=False,
    )
```

time: 191 us -> 63 us (0.33)
  between operations: 60.3 us -> 0.13 us
  matrix products: 54.4 us -> 0 us
  local copies, waits for them, and re-layouts: 26.5 us -> 0.02 us
  Pallas kernels: 0 us -> 26 us
  other arithmetic: 21.3 us -> 0.7 us
  starting transfers between devices: 26.8 us -> 35.3 us
    dot_general x31 -> x0, matrix products: 54.4 us -> none  [the longest x5 40.2 us: per_device(): jnp.dot(source.reshape(depth * tile_rows, model_width), w_keyval, preferr...]
    slice x36 -> x0, local copies, waits for them, and re-layouts: 26.1 us -> none  [the longest x13 14 us: attend_one(): key_heads = tile[:, :model_width].reshape(tile_rows, HEADS, head_size)]
    pallas_call x0 -> x6, Pallas kernels: none -> 26 us  [the longest x1 9.19 us: per_device(): pl.pallas_call(own_kernel, out_shape=[stat, stat, mix], in_specs=[SMEM, S...]
    select_n x8 -> x1, other arithmetic: 17.3 us -> 0.7 us  [per_device(): wanted = jnp.where(neighbour_live > 0, neighbour_tiles, -1)]
    ppermute x4 -> x8, starting transfers between devices: 26.8 us -> 35.3 us  [the longest x4 29.3 us: to_sources(): return lax.ppermute(block, 'nodes', [(i, source(i, n)) for i in range(n)])]
    convert_element_type x2 -> x0, other arithmetic: 2.27 us -> none  [attend_one(): weights = (raised / row_total).astype(jnp.bfloat16)]
  transfers between devices with their start and end apart: 4 -> 8, of which waited for: 0 -> 1; matrix products, arithmetic and copies ran while one was open for 21% -> 0% of each run, Pallas kernels for 0% -> 33%
where the time goes in v1:
time: 63 us; the launch traced here: 62.9 us
  starting transfers between devices  35.3 us (56%)
  Pallas kernels  26 us (41%)
  waiting for transfers between devices  0.82 us (1%)
  other arithmetic  0.7 us (1%)
    ppermute x4, starting transfers between devices, to_sources(): return lax.ppermute(block, 'nodes', [(i, source(i, n)) for i in range(n)])  29.3 us
    pallas_call x1, Pallas kernels, per_device(): pl.pallas_call(own_kernel, out_shape=[stat, stat, mix], in_specs=[SMEM, S...  9.19 us
    pallas_call x2, Pallas kernels, per_device(): pl.pallas_call(functools.partial(chunk_kernel, sources, own), out_shape=[...  7.84 us
    ppermute x4, starting transfers between devices, from_sources(): return lax.ppermute(block, 'nodes', [(source(i, n), i) for i in range(n)])  5.98 us
    pallas_call x1, Pallas kernels, per_device(): pl.pallas_call(functools.partial(last_kernel, [SOURCES[LAST]], own), out_...  4.43 us
    pallas_call x1, Pallas kernels, per_device(): pl.pallas_call(front_kernel, out_shape=[query, jax.ShapeDtypeStruct(store...  3.67 us
  transfers between devices with their start and end apart: 8, of which 1 were waited for; matrix products, arithmetic and copies ran while one was open for 0% of the time, Pallas kernels for 33%

profile of v1, /device:TPU:40, one launch (start us, length us, event | category | flops | bytes accessed | tf_op | source)
XLA Modules:
  0.0 62.9 jit_solution(18063465335732705756)
XLA Ops:
  0.0 0.7 %compare_select_fusion = s32[2,6]{1,0:T(2,128)S(1)} fusion(s32[2,6]{1,0:T(2,128)} %tiles_ref.7, s32[2,6]{1,0:T(2,128)} %live_ref.7), kind=kLoop, calls=%fused_computation | loop fusion | flops 24 | bytes 144 | tf_op jit(solution)/shard_map/jit(_where)/select_n | solution.py:295
  0.7 25.0 %collective-permute-start = (s32[2,6]{1,0:T(2,128)S(1)}, s32[2,6]{1,0:T(2,128)S(1)}, u32[]{:S(2)}, u32[]{:S(2)}) collective-permute-start(s32[2,6]{1,0:T(2,128)S(1)} %compare_select_fusion), channel_id=1, source_target_pairs={{0,126},{1,127},{2,0},{3,1},{4,2},{5,3},{6,4},{7,5},{8,6},{9,7},{1... | collective-permute-start | bytes 152 | tf_op jit(solution)/shard_map/ppermute | solution.py:284
  25.7 0.0 collective-permute-start.1
  25.7 4.3 %collective-permute-start.2 = (s32[2,6]{1,0:T(2,128)S(1)}, s32[2,6]{1,0:T(2,128)S(1)}, u32[]{:S(2)}, u32[]{:S(2)}) collective-permute-start(s32[2,6]{1,0:T(2,128)S(1)} %compare_select_fusion), channel_id=1, source_target_pairs={{0,127},{1,2},{2,1},{3,4},{4,3},{5,6},{6,5},{7,8},{8,7},{9,10},{10... | collective-permute-start | bytes 152 | tf_op jit(solution)/shard_map/ppermute | solution.py:284
  30.0 0.0 collective-permute-start.3
  30.0 3.7 %front.1 = (bf16[2,8,128,256]{3,2,1,0:T(8,128)(2,1)S(1)}, bf16[8,128,1024]{2,1,0:T(8,128)(2,1)S(1)}, bf16[1024,2048]{1,0:T(8,128)(2,1)S(1)}) custom-call(bf16[256,1024]{1,0:T(8,128)(2,1)} %mesh.1, bf16[1024,1024]{1,0:T(8,128)(2,1)} %w_query_hbm.1, bf16[8,128,1024]{2,1,0:T(8,128)(2,1)} %bitcast.11, bf16[1024,2048]{1,0:T(8,128)(2,1)} %w_keyval_hbm.1), custom_call_target="tpu_custom_call" | custom-call | flops 1000000000 | bytes 10000000 | tf_op jit(solution)/shard_map/front/pallas_call | solution.py:308
  33.7 0.0 copy-start.1
  33.7 0.0 copy-start.2
  33.7 0.0 collective-permute-done.refs_0_
  33.7 0.0 collective-permute-done.1.refs_1_
  33.7 0.0 collective-permute-done.2.refs_2_
  33.7 0.0 collective-permute-done.3.refs_3_
  33.7 0.8 %pack.1 = (bf16[2,128,1024]{2,1,0:T(8,128)(2,1)S(1)}, bf16[2,128,1024]{2,1,0:T(8,128)(2,1)S(1)}, bf16[2,128,1024]{2,1,0:T(8,128)(2,1)S(1)}, bf16[2,128,1024]{2,1,0:T(8,128)(2,1)S(1)}) custom-call(s32[2,6]{1,0:T(2,128)S(1)} %collective-permute-done.refs_0_, s32[2,6]{1,0:T(2,128)S(1)} %collective-permute-done.1.refs_1_, ...), custom_call_target="tpu_custom_call" | custom-call | tf_op jit(solution)/shard_map/pack/pallas_call | solution.py:75
  34.6 0.6 %collective-permute-start.4 = (bf16[2,128,1024]{2,1,0:T(8,128)(2,1)S(1)}, bf16[2,128,1024]{2,1,0:T(8,128)(2,1)S(1)}, u32[]{:S(2)}, u32[]{:S(2)}) collective-permute-start(bf16[2,128,1024]{2,1,0:T(8,128)(2,1)S(1)} %get-tuple-element.27), channel_id=1, source_target_pairs={{1,0},{0,1},{3,2},{2,3},{5,4},{4,5},{7,6},{6,7},{9,8},{8,9},{11,10... | collective-permute-start | bytes 1572872 | tf_op jit(solution)/shard_map/ppermute | solution.py:287
  35.2 0.0 collective-permute-start.5
  35.2 5.3 %collective-permute-start.6 = (bf16[2,128,1024]{2,1,0:T(8,128)(2,1)S(1)}, bf16[2,128,1024]{2,1,0:T(8,128)(2,1)S(1)}, u32[]{:S(2)}, u32[]{:S(2)}) collective-permute-start(bf16[2,128,1024]{2,1,0:T(8,128)(2,1)S(1)} %get-tuple-element.32), channel_id=1, source_target_pairs={{2,0},{3,1},{4,2},{5,3},{6,4},{7,5},{8,6},{9,7},{10,8},{11,9},{12,... | collective-permute-start | bytes 1572872 | tf_op jit(solution)/shard_map/ppermute | solution.py:287
  40.5 0.0 collective-permute-start.7
  40.5 9.2 %own.1 = (f32[2,8,256]{2,1,0:T(8,128)S(1)}, f32[2,8,256]{2,1,0:T(8,128)S(1)}, f32[2,1024,128]{2,1,0:T(8,128)S(1)}) custom-call(s32[2,6]{1,0:T(2,128)S(1)} %copy-done.1, s32[2,6]{1,0:T(2,128)S(1)} %copy-done.2, bf16[1024,1024]{1,0:T(8,128)(2,1)S(1)} %bitcast.6, bf16[1024,2048]{1,0:T(8,128)(2,1)S(1)} %get-tuple-element.21.w_keyval, ...), custom_call_target="tpu_custom_call" | custom-call | flops 6000000000 | bytes 10000000 | tf_op jit(solution)/shard_map/own/pallas_call | solution.py:326
  49.7 0.0 collective-permute-done.4
  49.8 2.7 %chunk.2 = (f32[2,8,256]{2,1,0:T(8,128)S(1)}, f32[2,8,256]{2,1,0:T(8,128)S(1)}, f32[2,1024,128]{2,1,0:T(8,128)S(1)}) custom-call(s32[2,6]{1,0:T(2,128)S(1)} %copy-done.1, s32[2,6]{1,0:T(2,128)S(1)} %copy-done.2, bf16[1024,2048]{1,0:T(8,128)(2,1)S(1)} %get-tuple-element.21.w_keyval, ...), custom_call_target="tpu_custom_call", output_to_operand_aliasing={{0}: (4, {}), {1}: (5, {}), {2}: (6, {})} | custom-call | flops 2000000000 | bytes 1000000 | tf_op jit(solution)/shard_map/chunk/pallas_call | solution.py:340
  52.5 0.8 %collective-permute-done.5 = bf16[2,128,1024]{2,1,0:T(8,128)(2,1)S(1)} collective-permute-done((bf16[2,128,1024]{2,1,0:T(8,128)(2,1)S(1)}, bf16[2,128,1024]{2,1,0:T(8,128)(2,1)S(1)}, u32[]{:S(2)}, u32[]{:S(2)}) %collective-permute-start.5) | collective-permute-done | bytes 524320 | tf_op jit(solution)/shard_map/ppermute | solution.py:287
  53.3 0.0 collective-permute-done.6
  53.3 5.1 %chunk.3 = (f32[2,8,256]{2,1,0:T(8,128)S(1)}, f32[2,8,256]{2,1,0:T(8,128)S(1)}, f32[2,1024,128]{2,1,0:T(8,128)S(1)}) custom-call(s32[2,6]{1,0:T(2,128)S(1)} %copy-done.1, s32[2,6]{1,0:T(2,128)S(1)} %copy-done.2, bf16[1024,2048]{1,0:T(8,128)(2,1)S(1)} %get-tuple-element.21.w_keyval, ...), custom_call_target="tpu_custom_call", output_to_operand_aliasing={{0}: (4, {}), {1}: (5, {}), {2}: (6, {})} | custom-call | flops 2000000000 | bytes 1000000 | tf_op jit(solution)/shard_map/chunk/pallas_call | solution.py:340
  58.4 4.4 %last.1 = f32[256,1024]{1,0:T(8,128)} custom-call(s32[2,6]{1,0:T(2,128)S(1)} %copy-done.1, s32[2,6]{1,0:T(2,128)S(1)} %copy-done.2, bf16[1024,2048]{1,0:T(8,128)(2,1)S(1)} %get-tuple-element.21.w_keyval, bf16[2,8,128,256]{3,2,1,0:T(8,128)(2,1)S(1)} %get-tuple-element.22.queries, f32[2,8,256]{2,1,0:T(8,128)S(1)} %get-tuple-element.33.tops_in, ...), custom_call_target="tpu_custom_call" | custom-call | flops 3000000000 | bytes 1000000 | tf_op jit(solution)/shard_map/last/pallas_call | solution.py:355
  (7 shorter events, 0.0 us)
Async XLA Ops:
  0.7 33.0 %collective-permute-start = (s32[2,6]{1,0:T(2,128)S(1)}, s32[2,6]{1,0:T(2,128)S(1)}, u32[]{:S(2)}, u32[]{:S(2)}) collective-permute-start(s32[2,6]{1,0:T(2,128)S(1)} %compare_select_fusion), channel_id=1, source_target_pairs={{0,126},{1,127},{2,0},{3,1},{4,2},{5,3},{6,4},{7,5},{8,6},{9,7},{1... | collective-permute-start | bytes 152 | tf_op jit(solution)/shard_map/ppermute | solution.py:284
  25.7 8.0 %collective-permute-start.1 = (s32[2,6]{1,0:T(2,128)S(1)}, s32[2,6]{1,0:T(2,128)S(1)}, u32[]{:S(2)}, u32[]{:S(2)}) collective-permute-start(s32[2,6]{1,0:T(2,128)S(1)} %compare_select_fusion), channel_id=1, source_target_pairs={{0,2},{1,3},{2,4},{3,5},{4,6},{5,7},{6,8},{7,9},{8,10},{9,11},{10,... | collective-permute-start | bytes 152 | tf_op jit(solution)/shard_map/ppermute | solution.py:284
  25.7 8.0 %collective-permute-start.2 = (s32[2,6]{1,0:T(2,128)S(1)}, s32[2,6]{1,0:T(2,128)S(1)}, u32[]{:S(2)}, u32[]{:S(2)}) collective-permute-start(s32[2,6]{1,0:T(2,128)S(1)} %compare_select_fusion), channel_id=1, source_target_pairs={{0,127},{1,2},{2,1},{3,4},{4,3},{5,6},{6,5},{7,8},{8,7},{9,10},{10... | collective-permute-start | bytes 152 | tf_op jit(solution)/shard_map/ppermute | solution.py:284
  30.0 3.7 %collective-permute-start.3 = (s32[2,6]{1,0:T(2,128)S(1)}, s32[2,6]{1,0:T(2,128)S(1)}, u32[]{:S(2)}, u32[]{:S(2)}) collective-permute-start(s32[2,6]{1,0:T(2,128)S(1)} %compare_select_fusion), channel_id=1, source_target_pairs={{0,1},{1,0},{2,3},{3,2},{4,5},{5,4},{6,7},{7,6},{8,9},{9,8},{10,11... | collective-permute-start | bytes 152 | tf_op jit(solution)/shard_map/ppermute | solution.py:284
  33.7 6.9 %copy-start.1 = (s32[2,6]{1,0:T(2,128)S(1)}, s32[2,6]{1,0:T(2,128)}, u32[]{:S(2)}) copy-start(s32[2,6]{1,0:T(2,128)} %tiles_ref.7) | copy-start | bytes 148
  33.7 6.9 %copy-start.2 = (s32[2,6]{1,0:T(2,128)S(1)}, s32[2,6]{1,0:T(2,128)}, u32[]{:S(2)}) copy-start(s32[2,6]{1,0:T(2,128)} %live_ref.7) | copy-start | bytes 148
  34.6 15.2 %collective-permute-start.4 = (bf16[2,128,1024]{2,1,0:T(8,128)(2,1)S(1)}, bf16[2,128,1024]{2,1,0:T(8,128)(2,1)S(1)}, u32[]{:S(2)}, u32[]{:S(2)}) collective-permute-start(bf16[2,128,1024]{2,1,0:T(8,128)(2,1)S(1)} %get-tuple-element.27), channel_id=1, source_target_pairs={{1,0},{0,1},{3,2},{2,3},{5,4},{4,5},{7,6},{6,7},{9,8},{8,9},{11,10... | collective-permute-start | bytes 1572872 | tf_op jit(solution)/shard_map/ppermute | solution.py:287
  35.2 18.1 %collective-permute-start.5 = (bf16[2,128,1024]{2,1,0:T(8,128)(2,1)S(1)}, bf16[2,128,1024]{2,1,0:T(8,128)(2,1)S(1)}, u32[]{:S(2)}, u32[]{:S(2)}) collective-permute-start(bf16[2,128,1024]{2,1,0:T(8,128)(2,1)S(1)} %get-tuple-element.31), channel_id=1, source_target_pairs={{126,0},{127,1},{0,2},{1,3},{2,4},{3,5},{4,6},{5,7},{6,8},{7,9},{8... | collective-permute-start | bytes 1572872 | tf_op jit(solution)/shard_map/ppermute | solution.py:287
  35.2 18.1 %collective-permute-start.6 = (bf16[2,128,1024]{2,1,0:T(8,128)(2,1)S(1)}, bf16[2,128,1024]{2,1,0:T(8,128)(2,1)S(1)}, u32[]{:S(2)}, u32[]{:S(2)}) collective-permute-start(bf16[2,128,1024]{2,1,0:T(8,128)(2,1)S(1)} %get-tuple-element.32), channel_id=1, source_target_pairs={{2,0},{3,1},{4,2},{5,3},{6,4},{7,5},{8,6},{9,7},{10,8},{11,9},{12,... | collective-permute-start | bytes 1572872 | tf_op jit(solution)/shard_map/ppermute | solution.py:287
  40.5 17.9 %collective-permute-start.7 = (bf16[2,128,1024]{2,1,0:T(8,128)(2,1)S(1)}, bf16[2,128,1024]{2,1,0:T(8,128)(2,1)S(1)}, u32[]{:S(2)}, u32[]{:S(2)}) collective-permute-start(bf16[2,128,1024]{2,1,0:T(8,128)(2,1)S(1)} %get-tuple-element.36), channel_id=1, source_target_pairs={{127,0},{2,1},{1,2},{4,3},{3,4},{6,5},{5,6},{8,7},{7,8},{10,9},{9,... | collective-permute-start | bytes 1572872 | tf_op jit(solution)/shard_map/ppermute | solution.py:287
  53.3 5.1 %copy-start = (bf16[256,1024]{1,0:T(8,128)(2,1)S(1)}, bf16[256,1024]{1,0:T(8,128)(2,1)}, u32[]{:S(2)}) copy-start(bf16[256,1024]{1,0:T(8,128)(2,1)} %mesh.1) | copy-start | bytes 1572868
  53.3 5.1 %copy-start.3 = (bf16[1024,1024]{1,0:T(8,128)(2,1)S(1)}, bf16[1024,1024]{1,0:T(8,128)(2,1)}, u32[]{:S(2)}) copy-start(bf16[1024,1024]{1,0:T(8,128)(2,1)} %w_out.1) | copy-start | bytes 6291460

commit v2 on v1

--- a/solution.py
+++ b/solution.py
@@ -28,6 +28,10 @@
     return (i + n - 1 + 2 * (i % 2)) % n
 
 
+def relay_of(i, n):
+    return (i + n - REACH + 2 * REACH * (i % 2)) % n
+
+
 def ahead_of(i, n):
     return (i + REACH) % n
 
@@ -36,8 +40,8 @@
     return (i + n - REACH) % n
 
 
-SOURCES = (behind_of, ahead_of, cross_of, partner_of)
-STAGES = ((3,), (0, 1))
+SOURCES = (behind_of, ahead_of, cross_of)
+STAGES = ((0, 1),)
 LAST = 2
 
 
@@ -56,29 +60,38 @@
     return [ref[i, j] for i in range(ref.shape[0]) for j in range(ref.shape[1])]
 
 
-def pack_kernel(*refs):
-    count = len(SOURCES)
-    asked, grid, outs = refs[:count], refs[count], refs[count + 1 :]
+def copy_listed(listed, base, grid, out):
     own = grid.shape[0]
+    low, high = span_of(listed, base, own)
+    out[0] = grid[jnp.where(high < 0, 0, low)]
+    out[1] = grid[jnp.maximum(high, 0)]
+
+
+def pack_kernel(from_ahead, from_behind, grid, to_ahead, to_behind):
+    base = lax.axis_index("nodes") * grid.shape[0]
+    copy_listed(entries(from_ahead), base, grid, to_ahead)
+    copy_listed(entries(from_behind), base, grid, to_behind)
+
+
+def relay_kernel(from_ahead, from_behind, grid, out):
     me = lax.axis_index("nodes")
-    for c in range(count):
-        low, high = span_of(entries(asked[c]), me * own, own)
-        low = jnp.where(high < 0, 0, low)
-        high = jnp.maximum(high, 0)
-        outs[c][0] = grid[low]
-        outs[c][1] = grid[high]
-
-
-def pack(asked, grid):
-    count = len(SOURCES)
+    base = partner_of(me, lax.axis_size("nodes")) * grid.shape[0]
+    even = me % 2 == 0
+    listed = [
+        jnp.where(even, ahead, behind)
+        for ahead, behind in zip(entries(from_ahead), entries(from_behind))
+    ]
+    copy_listed(listed, base, grid, out)
+
+
+def pack(kernel, count, asked, grid):
     shape = jax.ShapeDtypeStruct((CAP,) + grid.shape[1:], grid.dtype)
     return pl.pallas_call(
-        pack_kernel,
+        kernel,
         out_shape=[shape] * count,
-        in_specs=[SMEM] * count + [VMEM],
+        in_specs=[SMEM, SMEM, VMEM],
         out_specs=[VMEM] * count,
         compiler_params=pltpu.CompilerParams(vmem_limit_bytes=4 * MIB),
-        name="pack",
     )(*asked, grid)
 
 
@@ -159,28 +172,23 @@
     lax.fori_loop(0, count * mesh_tiles, body, 0)
 
 
-def front_kernel(mesh_hbm, w_query_hbm, grid_hbm, w_keyval_hbm, queries, grid, w_keyval, mesh, w_query, sems):
+def front_kernel(mesh_hbm, w_query_hbm, queries, mesh, w_query, sems):
     model_width = w_query.shape[0]
     width = queries.shape[2]
     head = width // 2
     step = 256
-    copies = [
-        pltpu.make_async_copy(source, target, sems.at[k])
-        for k, (source, target) in enumerate(
-            (
-                (mesh_hbm, mesh),
-                (w_query_hbm, w_query),
-                (grid_hbm, grid),
-                (w_keyval_hbm, w_keyval),
-            )
+    copies = [pltpu.make_async_copy(mesh_hbm, mesh, sems.at[0])]
+    for k, column in enumerate(range(0, model_width, step)):
+        columns = pl.ds(column, step)
+        copies.append(
+            pltpu.make_async_copy(w_query_hbm.at[:, columns], w_query.at[:, columns], sems.at[k + 1])
         )
-    ]
     for copy in copies:
         copy.start()
     queries[...] = jnp.zeros(queries.shape, queries.dtype)
     copies[0].wait()
-    copies[1].wait()
-    for column in range(0, model_width, step):
+    for n, column in enumerate(range(0, model_width, step)):
+        copies[n + 1].wait()
         part = jnp.dot(
             mesh[...], w_query[:, column : column + step], preferred_element_type=jnp.float32
         )
@@ -192,22 +200,70 @@
                 queries[m, which // 2, k * head : (k + 1) * head, k * TILE : (k + 1) * TILE] = turned[
                     h * head : (h + 1) * head, m * TILE : (m + 1) * TILE
                 ]
-    copies[2].wait()
-    copies[3].wait()
-
-
-def own_kernel(tiles_ref, live_ref, grid, w_keyval, queries, tops, totals, mixed, keys, values):
+
+
+def own_kernel(tiles_ref, live_ref, grid, beside, w_keyval, queries, tops, totals, mixed, rows, keys, values, found):
     own = grid.shape[0] // TILE
+    mesh_tiles = tiles_ref.shape[0]
     tops[...] = jnp.full(tops.shape, LOW, jnp.float32)
     totals[...] = jnp.zeros(totals.shape, jnp.float32)
     mixed[...] = jnp.zeros(mixed.shape, jnp.float32)
-    project(grid, w_keyval, keys, values, w_keyval.shape[0])
-    base = lax.axis_index("nodes") * own
-
-    def keep(tile):
-        return base + tile, jnp.bool_(True)
-
-    add_listed(own, keep, tiles_ref, live_ref, keys, values, queries, tops, totals, mixed)
+    me = lax.axis_index("nodes")
+    base = me * own
+    base_beside = partner_of(me, lax.axis_size("nodes")) * own
+    masks = []
+    for m in range(mesh_tiles):
+        mask = jnp.int32(0)
+        for j in range(tiles_ref.shape[1]):
+            tile = tiles_ref[m, j]
+            here = tile - base
+            there = tile - base_beside
+            bit = jnp.where((here >= 0) & (here < own), here, -1)
+            bit = jnp.where((there >= 0) & (there < own), there + own, bit)
+            taken = (live_ref[m, j] > 0) & (bit >= 0)
+            mask = mask | jnp.where(taken, lax.shift_left(jnp.int32(1), jnp.maximum(bit, 0)), 0)
+        masks.append(mask)
+    union = functools.reduce(jnp.bitwise_or, masks)
+    count = jnp.int32(0)
+    for bit in range(2 * own):
+        found[count] = jnp.int32(bit)
+        count = count + ((union >> bit) & 1)
+    found[count] = jnp.int32(0)
+    group = rows.shape[0] // TILE
+
+    def body(g, carry):
+        for k in range(group):
+            bit = found[g * group + k]
+            place = slice(k * TILE, (k + 1) * TILE)
+
+            @pl.when(bit < own)
+            def _():
+                rows[place, :] = grid[pl.ds(pl.multiple_of(bit * TILE, TILE), TILE), :]
+
+            @pl.when(bit >= own)
+            def _():
+                rows[place, :] = beside[pl.ds(pl.multiple_of((bit - own) * TILE, TILE), TILE), :]
+
+        project(rows, w_keyval, keys, values, w_keyval.shape[0])
+
+        def visit(i, inner):
+            k = i // mesh_tiles
+            m = i % mesh_tiles
+            place = g * group + k
+            mask = masks[0]
+            for other in range(1, mesh_tiles):
+                mask = jnp.where(m == other, masks[other], mask)
+            taken = (lax.shift_right_logical(mask, found[place]) & 1) > 0
+
+            @pl.when(taken & (place < count))
+            def _():
+                add_tile(k, m, keys, values, queries, tops, totals, mixed)
+
+            return inner
+
+        return lax.fori_loop(0, group * mesh_tiles, visit, carry)
+
+    lax.fori_loop(0, (count + group - 1) // group, body, 0)
 
 
 def chunk_update(sources, own, tiles_ref, live_ref, rows_ref, w_keyval, keys, values, *state):
@@ -294,45 +350,55 @@
 
     wanted = jnp.where(neighbour_live > 0, neighbour_tiles, -1)
     asked = []
-    for source in SOURCES:
+    for source in (behind_of, ahead_of):
         asked.append(to_sources(wanted, source))
+    tiled = grid_latents.reshape(own, TILE, model_width)
+    beside = from_sources(tiled, partner_of)
     stored = [
         pltpu.with_memory_space_constraint(array, pltpu.HBM)
-        for array in (
-            mesh_latents,
-            w_query,
-            grid_latents.reshape(own, TILE, model_width),
-            w_keyval,
-        )
+        for array in (mesh_latents, w_query)
     ]
-    queries, grid, w_kv = pl.pallas_call(
+    queries = pl.pallas_call(
         front_kernel,
-        out_shape=[query, jax.ShapeDtypeStruct(stored[2].shape, bf16), jax.ShapeDtypeStruct(w_keyval.shape, bf16)],
-        in_specs=[HBM] * 4,
-        out_specs=[VMEM] * 3,
+        out_shape=query,
+        in_specs=[HBM] * 2,
+        out_specs=VMEM,
         scratch_shapes=[
             pltpu.VMEM(mesh_latents.shape, bf16),
             pltpu.VMEM(w_query.shape, bf16),
-            pltpu.SemaphoreType.DMA((4,)),
+            pltpu.SemaphoreType.DMA((1 + model_width // 256,)),
         ],
         compiler_params=pltpu.CompilerParams(vmem_limit_bytes=8 * MIB),
-        cost_estimate=pl.CostEstimate(flops=10**9, transcendentals=0, bytes_accessed=10**7),
+        cost_estimate=pl.CostEstimate(flops=3 * 10**9, transcendentals=0, bytes_accessed=10**7),
         name="front",
     )(*stored)
-    packed = pack(asked, grid)
+    packed = pack(pack_kernel, 2, asked, tiled)
+    packed += pack(relay_kernel, 1, asked, beside)
     chunks = []
-    for block, source in zip(packed, SOURCES):
+    for block, source in zip(packed, (behind_of, ahead_of, relay_of)):
         chunks.append(from_sources(block, source).reshape(CAP * TILE, model_width))
     tops, totals, mixed = pl.pallas_call(
         own_kernel,
         out_shape=[stat, stat, mix],
-        in_specs=[SMEM, SMEM, VMEM, VMEM, VMEM],
+        in_specs=[SMEM, SMEM] + [VMEM] * 4,
         out_specs=[VMEM] * 3,
-        scratch_shapes=[pltpu.VMEM((own * TILE, model_width), bf16), pltpu.VMEM((own, model_width, TILE), bf16)],
-        compiler_params=pltpu.CompilerParams(vmem_limit_bytes=16 * MIB),
+        scratch_shapes=[
+            pltpu.VMEM((CAP * TILE, model_width), bf16),
+            pltpu.VMEM((CAP * TILE, model_width), bf16),
+            pltpu.VMEM((CAP, model_width, TILE), bf16),
+            pltpu.SMEM((2 * own + 1,), jnp.int32),
+        ],
+        compiler_params=pltpu.CompilerParams(vmem_limit_bytes=12 * MIB),
         cost_estimate=pl.CostEstimate(flops=6 * 10**9, transcendentals=0, bytes_accessed=10**7),
         name="own",
-    )(neighbour_tiles, neighbour_live, grid.reshape(own * TILE, model_width), w_kv, queries)
+    )(
+        neighbour_tiles,
+        neighbour_live,
+        grid_latents,
+        beside.reshape(own * TILE, model_width),
+        w_keyval,
+        queries,
+    )
 
     for members in STAGES:
         sources = [SOURCES[c] for c in members]
@@ -351,7 +417,7 @@
             compiler_params=pltpu.CompilerParams(vmem_limit_bytes=12 * MIB),
             cost_estimate=pl.CostEstimate(flops=2 * 10**9, transcendentals=0, bytes_accessed=10**6),
             name="chunk",
-        )(neighbour_tiles, neighbour_live, w_kv, queries, tops, totals, mixed, *[chunks[c] for c in members])
+        )(neighbour_tiles, neighbour_live, w_keyval, queries, tops, totals, mixed, *[chunks[c] for c in members])
     return pl.pallas_call(
         functools.partial(last_kernel, [SOURCES[LAST]], own),
         out_shape=jax.ShapeDtypeStruct(mesh_latents.shape, f32),
@@ -365,7 +431,7 @@
         compiler_params=pltpu.CompilerParams(vmem_limit_bytes=12 * MIB),
         cost_estimate=pl.CostEstimate(flops=3 * 10**9, transcendentals=0, bytes_accessed=10**6),
         name="last",
-    )(neighbour_tiles, neighbour_live, w_kv, queries, tops, totals, mixed, chunks[LAST], mesh_latents, w_out)
+    )(neighbour_tiles, neighbour_live, w_keyval, queries, tops, totals, mixed, chunks[LAST], mesh_latents, w_out)
 
 
 def solution(mesh):

time: 63 us -> 57.4 us (0.911)
  starting transfers between devices: 35.3 us -> 30.7 us
  Pallas kernels: 26 us -> 23.4 us
  waiting for transfers between devices: 0.82 us -> 2.31 us
    ppermute x4 -> x2, starting transfers between devices: 29.3 us -> 25.1 us  [to_sources(): return lax.ppermute(block, 'nodes', [(i, source(i, n)) for i in range(n)])]
    pallas_call x2 -> x1, Pallas kernels: 7.84 us -> 5.11 us  [per_device(): pl.pallas_call(functools.partial(chunk_kernel, sources, own), out_shape=[...]
    ppermute x4, waiting for transfers between devices: 0.81 us -> 2.3 us  [from_sources(): return lax.ppermute(block, 'nodes', [(source(i, n), i) for i in range(n)])]
    pallas_call x2 -> x3, Pallas kernels: 4.49 us -> 4.5 us  [the longest x1 3.17 us: per_device(): pl.pallas_call(front_kernel, out_shape=query, in_specs=[HBM] * 2, out_spe...]
  transfers between devices with their start and end apart: 8 -> 6, of which waited for: 1 -> 3; matrix products, arithmetic and copies ran while one was open for 0% -> 1% of each run, Pallas kernels for 33% -> 33%
where the time goes in v2:
time: 57.4 us; the launch traced here: 57.2 us
  starting transfers between devices  30.7 us (53%)
  Pallas kernels  23.4 us (41%)
  waiting for transfers between devices  2.31 us (4%)
  other arithmetic  0.7 us (1%)
    ppermute x2, starting transfers between devices, to_sources(): return lax.ppermute(block, 'nodes', [(i, source(i, n)) for i in range(n)])  25.1 us
    pallas_call x1, Pallas kernels, per_device(): pl.pallas_call(own_kernel, out_shape=[stat, stat, mix], in_specs=[SMEM, S...  9.39 us
    ppermute x4, starting transfers between devices, from_sources(): return lax.ppermute(block, 'nodes', [(source(i, n), i) for i in range(n)])  5.59 us
    pallas_call x1, Pallas kernels, per_device(): pl.pallas_call(functools.partial(chunk_kernel, sources, own), out_shape=[...  5.11 us
    pallas_call x1, Pallas kernels, per_device(): pl.pallas_call(functools.partial(last_kernel, [SOURCES[LAST]], own), out_...  4.38 us
    pallas_call x1, Pallas kernels, per_device(): pl.pallas_call(front_kernel, out_shape=query, in_specs=[HBM] * 2, out_spe...  3.17 us
    ppermute x4, waiting for transfers between devices, from_sources(): return lax.ppermute(block, 'nodes', [(source(i, n), i) for i in range(n)])  2.3 us
    pallas_call x2, Pallas kernels, pack(): pl.pallas_call(kernel, out_shape=[shape] * count, in_specs=[SMEM, SMEM, V...  1.34 us
  transfers between devices with their start and end apart: 6, of which 3 were waited for; matrix products, arithmetic and copies ran while one was open for 1% of the time, Pallas kernels for 33%

profile of v2, /device:TPU:40, one launch (start us, length us, event | category | flops | bytes accessed | tf_op | source)
XLA Modules:
  0.0 57.2 jit_solution(12647394808699638997)
XLA Ops:
  0.0 0.0 collective-permute-start
  0.0 0.7 %compare_select_fusion = s32[2,6]{1,0:T(2,128)S(1)} fusion(s32[2,6]{1,0:T(2,128)} %tiles_ref.5, s32[2,6]{1,0:T(2,128)} %live_ref.5), kind=kLoop, calls=%fused_computation | loop fusion | flops 24 | bytes 144 | tf_op jit(solution)/shard_map/jit(_where)/select_n | solution.py:351
  0.7 1.6 %collective-permute-start.2 = (s32[2,6]{1,0:T(2,128)S(1)}, s32[2,6]{1,0:T(2,128)S(1)}, u32[]{:S(2)}, u32[]{:S(2)}) collective-permute-start(s32[2,6]{1,0:T(2,128)S(1)} %compare_select_fusion), channel_id=1, source_target_pairs={{0,2},{1,3},{2,4},{3,5},{4,6},{5,7},{6,8},{7,9},{8,10},{9,11},{10,... | collective-permute-start | bytes 152 | tf_op jit(solution)/shard_map/ppermute | solution.py:340
  2.3 23.5 %collective-permute-start.1 = (s32[2,6]{1,0:T(2,128)S(1)}, s32[2,6]{1,0:T(2,128)S(1)}, u32[]{:S(2)}, u32[]{:S(2)}) collective-permute-start(s32[2,6]{1,0:T(2,128)S(1)} %compare_select_fusion), channel_id=1, source_target_pairs={{0,126},{1,127},{2,0},{3,1},{4,2},{5,3},{6,4},{7,5},{8,6},{9,7},{1... | collective-permute-start | bytes 152 | tf_op jit(solution)/shard_map/ppermute | solution.py:340
  25.8 3.2 %front.1.queries = bf16[2,8,128,256]{3,2,1,0:T(8,128)(2,1)S(1)} custom-call(bf16[256,1024]{1,0:T(8,128)(2,1)} %mesh.1, bf16[1024,1024]{1,0:T(8,128)(2,1)} %w_query_hbm.1), custom_call_target="tpu_custom_call" | custom-call | flops 3000000000 | bytes 10000000 | tf_op jit(solution)/shard_map/front/pallas_call | solution.py:361
  29.0 0.0 copy-start.1
  29.0 0.0 copy-start.2
  29.0 0.0 copy-start.3
  29.0 0.0 collective-permute-done.2.from_behind
  29.0 0.0 collective-permute-done.1.from_ahead
  29.0 0.0 copy-done
  29.0 0.7 %shard_map.73 = (bf16[2,128,1024]{2,1,0:T(8,128)(2,1)S(1)}, bf16[2,128,1024]{2,1,0:T(8,128)(2,1)S(1)}) custom-call(s32[2,6]{1,0:T(2,128)S(1)} %collective-permute-done.1.from_ahead, s32[2,6]{1,0:T(2,128)S(1)} %collective-permute-done.2.from_behind, bf16[8,128,1024]{2,1,0:T(8,128)(2,1)S(1)} %bitcast.6), custom_call_target="tpu_custom_call" | custom-call | tf_op jit(solution)/shard_map/pallas_call | solution.py:89
  29.7 0.1 collective-permute-start.3
  29.9 5.3 %collective-permute-start.4 = (bf16[2,128,1024]{2,1,0:T(8,128)(2,1)S(1)}, bf16[2,128,1024]{2,1,0:T(8,128)(2,1)S(1)}, u32[]{:S(2)}, u32[]{:S(2)}) collective-permute-start(bf16[2,128,1024]{2,1,0:T(8,128)(2,1)S(1)} %get-tuple-element.17), channel_id=1, source_target_pairs={{2,0},{3,1},{4,2},{5,3},{6,4},{7,5},{8,6},{9,7},{10,8},{11,9},{12,... | collective-permute-start | bytes 1572872 | tf_op jit(solution)/shard_map/ppermute | solution.py:343
  35.2 0.0 collective-permute-done.grid
  35.2 0.6 %shard_map.74 = bf16[2,128,1024]{2,1,0:T(8,128)(2,1)S(1)} custom-call(s32[2,6]{1,0:T(2,128)S(1)} %collective-permute-done.1.from_ahead, s32[2,6]{1,0:T(2,128)S(1)} %collective-permute-done.2.from_behind, bf16[8,128,1024]{2,1,0:T(8,128)(2,1)S(1)} %collective-permute-done.grid), custom_call_target="tpu_custom_call" | custom-call | tf_op jit(solution)/shard_map/pallas_call | solution.py:89
  35.9 0.1 collective-permute-start.5
  36.0 9.4 %own.1 = (f32[2,8,256]{2,1,0:T(8,128)S(1)}, f32[2,8,256]{2,1,0:T(8,128)S(1)}, f32[2,1024,128]{2,1,0:T(8,128)S(1)}) custom-call(s32[2,6]{1,0:T(2,128)S(1)} %copy-done.1, s32[2,6]{1,0:T(2,128)S(1)} %copy-done.2, bf16[1024,1024]{1,0:T(8,128)(2,1)S(1)} %copy-done, bf16[1024,1024]{1,0:T(8,128)(2,1)S(1)} %bitcast.7, bf16[1024,2048]{1,0:T(8,128)(2,1)S(1)} %copy-done.3, ...), custom_call_target="tpu_custom_call" | custom-call | flops 6000000000 | bytes 10000000 | tf_op jit(solution)/shard_map/own/pallas_call | solution.py:380
  45.4 1.8 %collective-permute-done.3 = bf16[2,128,1024]{2,1,0:T(8,128)(2,1)S(1)} collective-permute-done((bf16[2,128,1024]{2,1,0:T(8,128)(2,1)S(1)}, bf16[2,128,1024]{2,1,0:T(8,128)(2,1)S(1)}, u32[]{:S(2)}, u32[]{:S(2)}) %collective-permute-start.3) | collective-permute-done | bytes 524320 | tf_op jit(solution)/shard_map/ppermute | solution.py:343
  47.2 0.3 collective-permute-done.4
  47.5 5.1 %chunk.1 = (f32[2,8,256]{2,1,0:T(8,128)S(1)}, f32[2,8,256]{2,1,0:T(8,128)S(1)}, f32[2,1024,128]{2,1,0:T(8,128)S(1)}) custom-call(s32[2,6]{1,0:T(2,128)S(1)} %copy-done.1, s32[2,6]{1,0:T(2,128)S(1)} %copy-done.2, bf16[1024,2048]{1,0:T(8,128)(2,1)S(1)} %copy-done.3, ...), custom_call_target="tpu_custom_call", output_to_operand_aliasing={{0}: (4, {}), {1}: (5, {}), {2}: (6, {})} | custom-call | flops 2000000000 | bytes 1000000 | tf_op jit(solution)/shard_map/chunk/pallas_call | solution.py:406
  52.6 0.2 collective-permute-done.5
  52.8 0.0 copy-done.5
  52.8 4.4 %last.1 = f32[256,1024]{1,0:T(8,128)} custom-call(s32[2,6]{1,0:T(2,128)S(1)} %copy-done.1, s32[2,6]{1,0:T(2,128)S(1)} %copy-done.2, bf16[1024,2048]{1,0:T(8,128)(2,1)S(1)} %copy-done.3, bf16[2,8,128,256]{3,2,1,0:T(8,128)(2,1)S(1)} %front.1.queries, f32[2,8,256]{2,1,0:T(8,128)S(1)} %get-tuple-element.18.tops_in, ...), custom_call_target="tpu_custom_call" | custom-call | flops 3000000000 | bytes 1000000 | tf_op jit(solution)/shard_map/last/pallas_call | solution.py:421
  (7 shorter events, 0.0 us)
Async XLA Ops:
  0.0 35.2 %collective-permute-start = (bf16[8,128,1024]{2,1,0:T(8,128)(2,1)}, bf16[8,128,1024]{2,1,0:T(8,128)(2,1)S(1)}, u32[]{:S(2)}, u32[]{:S(2)}) collective-permute-start(bf16[8,128,1024]{2,1,0:T(8,128)(2,1)} %bitcast.5), channel_id=1, source_target_pairs={{1,0},{0,1},{3,2},{2,3},{5,4},{4,5},{7,6},{6,7},{9,8},{8,9},{11,10... | collective-permute-start | bytes 6291464 | tf_op jit(solution)/shard_map/ppermute | solution.py:343
  0.7 28.3 %copy-start = (bf16[1024,1024]{1,0:T(8,128)(2,1)S(1)}, bf16[1024,1024]{1,0:T(8,128)(2,1)}, u32[]{:S(2)}) copy-start(bf16[1024,1024]{1,0:T(8,128)(2,1)} %grid.1) | copy-start | bytes 6291460
  0.7 28.3 %collective-permute-start.2 = (s32[2,6]{1,0:T(2,128)S(1)}, s32[2,6]{1,0:T(2,128)S(1)}, u32[]{:S(2)}, u32[]{:S(2)}) collective-permute-start(s32[2,6]{1,0:T(2,128)S(1)} %compare_select_fusion), channel_id=1, source_target_pairs={{0,2},{1,3},{2,4},{3,5},{4,6},{5,7},{6,8},{7,9},{8,10},{9,11},{10,... | collective-permute-start | bytes 152 | tf_op jit(solution)/shard_map/ppermute | solution.py:340
  2.3 26.7 %collective-permute-start.1 = (s32[2,6]{1,0:T(2,128)S(1)}, s32[2,6]{1,0:T(2,128)S(1)}, u32[]{:S(2)}, u32[]{:S(2)}) collective-permute-start(s32[2,6]{1,0:T(2,128)S(1)} %compare_select_fusion), channel_id=1, source_target_pairs={{0,126},{1,127},{2,0},{3,1},{4,2},{5,3},{6,4},{7,5},{8,6},{9,7},{1... | collective-permute-start | bytes 152 | tf_op jit(solution)/shard_map/ppermute | solution.py:340
  29.0 7.0 %copy-start.1 = (s32[2,6]{1,0:T(2,128)S(1)}, s32[2,6]{1,0:T(2,128)}, u32[]{:S(2)}) copy-start(s32[2,6]{1,0:T(2,128)} %tiles_ref.5) | copy-start | bytes 148
  29.0 7.0 %copy-start.2 = (s32[2,6]{1,0:T(2,128)S(1)}, s32[2,6]{1,0:T(2,128)}, u32[]{:S(2)}) copy-start(s32[2,6]{1,0:T(2,128)} %live_ref.5) | copy-start | bytes 148
  29.0 7.0 %copy-start.3 = (bf16[1024,2048]{1,0:T(8,128)(2,1)S(1)}, bf16[1024,2048]{1,0:T(8,128)(2,1)}, u32[]{:S(2)}) copy-start(bf16[1024,2048]{1,0:T(8,128)(2,1)} %w_keyval.5) | copy-start | bytes 12582916
  29.7 17.5 %collective-permute-start.3 = (bf16[2,128,1024]{2,1,0:T(8,128)(2,1)S(1)}, bf16[2,128,1024]{2,1,0:T(8,128)(2,1)S(1)}, u32[]{:S(2)}, u32[]{:S(2)}) collective-permute-start(bf16[2,128,1024]{2,1,0:T(8,128)(2,1)S(1)} %get-tuple-element.16), channel_id=1, source_target_pairs={{126,0},{127,1},{0,2},{1,3},{2,4},{3,5},{4,6},{5,7},{6,8},{7,9},{8... | collective-permute-start | bytes 1572872 | tf_op jit(solution)/shard_map/ppermute | solution.py:343
  29.9 17.6 %collective-permute-start.4 = (bf16[2,128,1024]{2,1,0:T(8,128)(2,1)S(1)}, bf16[2,128,1024]{2,1,0:T(8,128)(2,1)S(1)}, u32[]{:S(2)}, u32[]{:S(2)}) collective-permute-start(bf16[2,128,1024]{2,1,0:T(8,128)(2,1)S(1)} %get-tuple-element.17), channel_id=1, source_target_pairs={{2,0},{3,1},{4,2},{5,3},{6,4},{7,5},{8,6},{9,7},{10,8},{11,9},{12,... | collective-permute-start | bytes 1572872 | tf_op jit(solution)/shard_map/ppermute | solution.py:343
  35.9 17.0 %collective-permute-start.5 = (bf16[2,128,1024]{2,1,0:T(8,128)(2,1)S(1)}, bf16[2,128,1024]{2,1,0:T(8,128)(2,1)S(1)}, u32[]{:S(2)}, u32[]{:S(2)}) collective-permute-start(bf16[2,128,1024]{2,1,0:T(8,128)(2,1)S(1)} %shard_map.74), channel_id=1, source_target_pairs={{126,0},{3,1},{0,2},{5,3},{2,4},{7,5},{4,6},{9,7},{6,8},{11,9},{8,... | collective-permute-start | bytes 1572872 | tf_op jit(solution)/shard_map/ppermute | solution.py:343
  47.5 5.3 %copy-start.4 = (bf16[1024,1024]{1,0:T(8,128)(2,1)S(1)}, bf16[1024,1024]{1,0:T(8,128)(2,1)}, u32[]{:S(2)}) copy-start(bf16[1024,1024]{1,0:T(8,128)(2,1)} %w_out.1) | copy-start | bytes 6291460
  47.5 5.3 %copy-start.5 = (bf16[256,1024]{1,0:T(8,128)(2,1)S(1)}, bf16[256,1024]{1,0:T(8,128)(2,1)}, u32[]{:S(2)}) copy-start(bf16[256,1024]{1,0:T(8,128)(2,1)} %mesh.1) | copy-start | bytes 1572868

commit v3 on v2

--- a/solution.py
+++ b/solution.py
@@ -92,6 +92,7 @@
         in_specs=[SMEM, SMEM, VMEM],
         out_specs=[VMEM] * count,
         compiler_params=pltpu.CompilerParams(vmem_limit_bytes=4 * MIB),
+        cost_estimate=pl.CostEstimate(flops=2 * 10**9, transcendentals=0, bytes_accessed=10**6),
     )(*asked, grid)
 
 
@@ -172,23 +173,26 @@
     lax.fori_loop(0, count * mesh_tiles, body, 0)
 
 
-def front_kernel(mesh_hbm, w_query_hbm, queries, mesh, w_query, sems):
-    model_width = w_query.shape[0]
-    width = queries.shape[2]
-    head = width // 2
-    step = 256
-    copies = [pltpu.make_async_copy(mesh_hbm, mesh, sems.at[0])]
-    for k, column in enumerate(range(0, model_width, step)):
-        columns = pl.ds(column, step)
-        copies.append(
-            pltpu.make_async_copy(w_query_hbm.at[:, columns], w_query.at[:, columns], sems.at[k + 1])
+def front_kernel(grid_hbm, grid, sems):
+    half = grid.shape[0] // 2
+    copies = [
+        pltpu.make_async_copy(
+            grid_hbm.at[pl.ds(k * half, half)], grid.at[pl.ds(k * half, half)], sems.at[k]
         )
+        for k in range(2)
+    ]
     for copy in copies:
         copy.start()
+    for copy in copies:
+        copy.wait()
+
+
+def form_queries(mesh, w_query, queries):
+    model_width = w_query.shape[0]
+    head = queries.shape[2] // 2
+    step = 256
     queries[...] = jnp.zeros(queries.shape, queries.dtype)
-    copies[0].wait()
-    for n, column in enumerate(range(0, model_width, step)):
-        copies[n + 1].wait()
+    for column in range(0, model_width, step):
         part = jnp.dot(
             mesh[...], w_query[:, column : column + step], preferred_element_type=jnp.float32
         )
@@ -202,9 +206,10 @@
                 ]
 
 
-def own_kernel(tiles_ref, live_ref, grid, beside, w_keyval, queries, tops, totals, mixed, rows, keys, values, found):
+def own_kernel(tiles_ref, live_ref, grid, beside, w_keyval, mesh, w_query, queries, tops, totals, mixed, rows, keys, values, found):
     own = grid.shape[0] // TILE
     mesh_tiles = tiles_ref.shape[0]
+    form_queries(mesh, w_query, queries)
     tops[...] = jnp.full(tops.shape, LOW, jnp.float32)
     totals[...] = jnp.zeros(totals.shape, jnp.float32)
     mixed[...] = jnp.zeros(mixed.shape, jnp.float32)
@@ -354,34 +359,27 @@
         asked.append(to_sources(wanted, source))
     tiled = grid_latents.reshape(own, TILE, model_width)
     beside = from_sources(tiled, partner_of)
-    stored = [
-        pltpu.with_memory_space_constraint(array, pltpu.HBM)
-        for array in (mesh_latents, w_query)
-    ]
-    queries = pl.pallas_call(
+    stored = pltpu.with_memory_space_constraint(tiled, pltpu.HBM)
+    near = pl.pallas_call(
         front_kernel,
-        out_shape=query,
-        in_specs=[HBM] * 2,
+        out_shape=jax.ShapeDtypeStruct(tiled.shape, bf16),
+        in_specs=[HBM],
         out_specs=VMEM,
-        scratch_shapes=[
-            pltpu.VMEM(mesh_latents.shape, bf16),
-            pltpu.VMEM(w_query.shape, bf16),
-            pltpu.SemaphoreType.DMA((1 + model_width // 256,)),
-        ],
-        compiler_params=pltpu.CompilerParams(vmem_limit_bytes=8 * MIB),
-        cost_estimate=pl.CostEstimate(flops=3 * 10**9, transcendentals=0, bytes_accessed=10**7),
+        scratch_shapes=[pltpu.SemaphoreType.DMA((2,))],
+        compiler_params=pltpu.CompilerParams(vmem_limit_bytes=4 * MIB),
+        cost_estimate=pl.CostEstimate(flops=10**8, transcendentals=0, bytes_accessed=10**6),
         name="front",
-    )(*stored)
-    packed = pack(pack_kernel, 2, asked, tiled)
+    )(stored)
+    packed = pack(pack_kernel, 2, asked, near)
     packed += pack(relay_kernel, 1, asked, beside)
     chunks = []
     for block, source in zip(packed, (behind_of, ahead_of, relay_of)):
         chunks.append(from_sources(block, source).reshape(CAP * TILE, model_width))
-    tops, totals, mixed = pl.pallas_call(
+    queries, tops, totals, mixed = pl.pallas_call(
         own_kernel,
-        out_shape=[stat, stat, mix],
-        in_specs=[SMEM, SMEM] + [VMEM] * 4,
-        out_specs=[VMEM] * 3,
+        out_shape=[query, stat, stat, mix],
+        in_specs=[SMEM, SMEM] + [VMEM] * 5,
+        out_specs=[VMEM] * 4,
         scratch_shapes=[
             pltpu.VMEM((CAP * TILE, model_width), bf16),
             pltpu.VMEM((CAP * TILE, model_width), bf16),
@@ -394,10 +392,11 @@
     )(
         neighbour_tiles,
         neighbour_live,
-        grid_latents,
+        near.reshape(own * TILE, model_width),
         beside.reshape(own * TILE, model_width),
         w_keyval,
-        queries,
+        mesh_latents,
+        w_query,
     )
 
     for members in STAGES:

time: 57.4 us -> 55.7 us (0.970)
  waiting for transfers between devices: 2.31 us -> 1.37 us
  Pallas kernels: 23.4 us -> 22.6 us
    ppermute x4, waiting for transfers between devices: 2.3 us -> 1.36 us  [from_sources(): return lax.ppermute(block, 'nodes', [(source(i, n), i) for i in range(n)])]
    pallas_call x2, Pallas kernels: 12.6 us -> 11.7 us  [the longest x1 10.1 us: per_device(): pl.pallas_call(own_kernel, out_shape=[query, stat, stat, mix], in_specs=[...]
  transfers between devices with their start and end apart: 6 -> 6, of which waited for: 3 -> 2; matrix products, arithmetic and copies ran while one was open for 1% -> 1% of each run, Pallas kernels for 33% -> 33%
where the time goes in v3:
time: 55.7 us; the launch traced here: 55.5 us
  starting transfers between devices  30.7 us (55%)
  Pallas kernels  22.6 us (41%)
  waiting for transfers between devices  1.37 us (2%)
  other arithmetic  0.7 us (1%)
    ppermute x2, starting transfers between devices, to_sources(): return lax.ppermute(block, 'nodes', [(i, source(i, n)) for i in range(n)])  25 us
    pallas_call x1, Pallas kernels, per_device(): pl.pallas_call(own_kernel, out_shape=[query, stat, stat, mix], in_specs=[...  10.1 us
    ppermute x4, starting transfers between devices, from_sources(): return lax.ppermute(block, 'nodes', [(source(i, n), i) for i in range(n)])  5.68 us
    pallas_call x1, Pallas kernels, per_device(): pl.pallas_call(functools.partial(chunk_kernel, sources, own), out_shape=[...  5.13 us
    pallas_call x1, Pallas kernels, per_device(): pl.pallas_call(functools.partial(last_kernel, [SOURCES[LAST]], own), out_...  4.46 us
    pallas_call x1, Pallas kernels, per_device(): pl.pallas_call(front_kernel, out_shape=jax.ShapeDtypeStruct(tiled.shape,...  1.56 us
    ppermute x4, waiting for transfers between devices, from_sources(): return lax.ppermute(block, 'nodes', [(source(i, n), i) for i in range(n)])  1.36 us
    pallas_call x2, Pallas kernels, pack(): pl.pallas_call(kernel, out_shape=[shape] * count, in_specs=[SMEM, SMEM, V...  1.34 us
  transfers between devices with their start and end apart: 6, of which 2 were waited for; matrix products, arithmetic and copies ran while one was open for 1% of the time, Pallas kernels for 33%

profile of v3, /device:TPU:40, one launch (start us, length us, event | category | flops | bytes accessed | tf_op | source)
XLA Modules:
  0.0 55.5 jit_solution(18189198618436666967)
XLA Ops:
  0.0 0.0 collective-permute-start
  0.0 0.7 %compare_select_fusion = s32[2,6]{1,0:T(2,128)S(1)} fusion(s32[2,6]{1,0:T(2,128)} %tiles_ref.5, s32[2,6]{1,0:T(2,128)} %live_ref.5), kind=kLoop, calls=%fused_computation | loop fusion | flops 24 | bytes 144 | tf_op jit(solution)/shard_map/jit(_where)/select_n | solution.py:356
  0.7 1.6 %collective-permute-start.2 = (s32[2,6]{1,0:T(2,128)S(1)}, s32[2,6]{1,0:T(2,128)S(1)}, u32[]{:S(2)}, u32[]{:S(2)}) collective-permute-start(s32[2,6]{1,0:T(2,128)S(1)} %compare_select_fusion), channel_id=1, source_target_pairs={{0,2},{1,3},{2,4},{3,5},{4,6},{5,7},{6,8},{7,9},{8,10},{9,11},{10,... | collective-permute-start | bytes 152 | tf_op jit(solution)/shard_map/ppermute | solution.py:345
  2.3 23.4 %collective-permute-start.1 = (s32[2,6]{1,0:T(2,128)S(1)}, s32[2,6]{1,0:T(2,128)S(1)}, u32[]{:S(2)}, u32[]{:S(2)}) collective-permute-start(s32[2,6]{1,0:T(2,128)S(1)} %compare_select_fusion), channel_id=1, source_target_pairs={{0,126},{1,127},{2,0},{3,1},{4,2},{5,3},{6,4},{7,5},{8,6},{9,7},{1... | collective-permute-start | bytes 152 | tf_op jit(solution)/shard_map/ppermute | solution.py:345
  25.7 1.6 %front.1.grid = bf16[8,128,1024]{2,1,0:T(8,128)(2,1)S(1)} custom-call(bf16[8,128,1024]{2,1,0:T(8,128)(2,1)} %bitcast.12), custom_call_target="tpu_custom_call" | custom-call | flops 100000000 | bytes 1000000 | tf_op jit(solution)/shard_map/front/pallas_call | solution.py:363
  27.3 0.0 collective-permute-done.2.from_behind
  27.3 0.0 collective-permute-done.1.from_ahead
  27.3 0.7 %shard_map.73 = (bf16[2,128,1024]{2,1,0:T(8,128)(2,1)S(1)}, bf16[2,128,1024]{2,1,0:T(8,128)(2,1)S(1)}) custom-call(s32[2,6]{1,0:T(2,128)S(1)} %collective-permute-done.1.from_ahead, s32[2,6]{1,0:T(2,128)S(1)} %collective-permute-done.2.from_behind, bf16[8,128,1024]{2,1,0:T(8,128)(2,1)S(1)} %front.1.grid), custom_call_target="tpu_custom_call" | custom-call | flops 2000000000 | bytes 1000000 | tf_op jit(solution)/shard_map/pallas_call | solution.py:89
  28.0 0.1 collective-permute-start.3
  28.1 0.0 copy-start
  28.1 0.0 copy-start.1
  28.1 0.0 copy-start.2
  28.1 0.0 copy-start.3
  28.2 0.0 copy-start.5
  28.2 5.4 %collective-permute-start.4 = (bf16[2,128,1024]{2,1,0:T(8,128)(2,1)S(1)}, bf16[2,128,1024]{2,1,0:T(8,128)(2,1)S(1)}, u32[]{:S(2)}, u32[]{:S(2)}) collective-permute-start(bf16[2,128,1024]{2,1,0:T(8,128)(2,1)S(1)} %get-tuple-element.19), channel_id=1, source_target_pairs={{2,0},{3,1},{4,2},{5,3},{6,4},{7,5},{8,6},{9,7},{10,8},{11,9},{12,... | collective-permute-start | bytes 1572872 | tf_op jit(solution)/shard_map/ppermute | solution.py:348
  33.6 0.0 collective-permute-done.grid
  33.6 0.6 %shard_map.74 = bf16[2,128,1024]{2,1,0:T(8,128)(2,1)S(1)} custom-call(s32[2,6]{1,0:T(2,128)S(1)} %collective-permute-done.1.from_ahead, s32[2,6]{1,0:T(2,128)S(1)} %collective-permute-done.2.from_behind, bf16[8,128,1024]{2,1,0:T(8,128)(2,1)S(1)} %collective-permute-done.grid), custom_call_target="tpu_custom_call" | custom-call | flops 2000000000 | bytes 1000000 | tf_op jit(solution)/shard_map/pallas_call | solution.py:89
  34.2 0.1 collective-permute-start.5
  34.4 10.1 %own.1 = (bf16[2,8,128,256]{3,2,1,0:T(8,128)(2,1)S(1)}, f32[2,8,256]{2,1,0:T(8,128)S(1)}, f32[2,8,256]{2,1,0:T(8,128)S(1)}, f32[2,1024,128]{2,1,0:T(8,128)S(1)}) custom-call(s32[2,6]{1,0:T(2,128)S(1)} %copy-done, s32[2,6]{1,0:T(2,128)S(1)} %copy-done.1, bf16[1024,1024]{1,0:T(8,128)(2,1)S(1)} %bitcast.6, bf16[1024,1024]{1,0:T(8,128)(2,1)S(1)} %bitcast.7, ...), custom_call_target="tpu_custom_call" | custom-call | flops 6000000000 | bytes 10000000 | tf_op jit(solution)/shard_map/own/pallas_call | solution.py:378
  44.6 0.9 %collective-permute-done.3 = bf16[2,128,1024]{2,1,0:T(8,128)(2,1)S(1)} collective-permute-done((bf16[2,128,1024]{2,1,0:T(8,128)(2,1)S(1)}, bf16[2,128,1024]{2,1,0:T(8,128)(2,1)S(1)}, u32[]{:S(2)}, u32[]{:S(2)}) %collective-permute-start.3) | collective-permute-done | bytes 524320 | tf_op jit(solution)/shard_map/ppermute | solution.py:348
  45.5 0.4 collective-permute-done.4
  45.9 5.1 %chunk.1 = (f32[2,8,256]{2,1,0:T(8,128)S(1)}, f32[2,8,256]{2,1,0:T(8,128)S(1)}, f32[2,1024,128]{2,1,0:T(8,128)S(1)}) custom-call(s32[2,6]{1,0:T(2,128)S(1)} %copy-done, s32[2,6]{1,0:T(2,128)S(1)} %copy-done.1, bf16[1024,2048]{1,0:T(8,128)(2,1)S(1)} %copy-done.2, ...), custom_call_target="tpu_custom_call", output_to_operand_aliasing={{0}: (4, {}), {1}: (5, {}), {2}: (6, {})} | custom-call | flops 2000000000 | bytes 1000000 | tf_op jit(solution)/shard_map/chunk/pallas_call | solution.py:405
  51.0 0.0 collective-permute-done.5
  51.1 4.5 %last.1 = f32[256,1024]{1,0:T(8,128)} custom-call(s32[2,6]{1,0:T(2,128)S(1)} %copy-done, s32[2,6]{1,0:T(2,128)S(1)} %copy-done.1, bf16[1024,2048]{1,0:T(8,128)(2,1)S(1)} %copy-done.2, bf16[2,8,128,256]{3,2,1,0:T(8,128)(2,1)S(1)} %get-tuple-element.14.queries, f32[2,8,256]{2,1,0:T(8,128)S(1)} %get-tuple-element.20.tops_in, ...), custom_call_target="tpu_custom_call" | custom-call | flops 3000000000 | bytes 1000000 | tf_op jit(solution)/shard_map/last/pallas_call | solution.py:420
  (7 shorter events, 0.0 us)
Async XLA Ops:
  0.0 33.6 %collective-permute-start = (bf16[8,128,1024]{2,1,0:T(8,128)(2,1)}, bf16[8,128,1024]{2,1,0:T(8,128)(2,1)S(1)}, u32[]{:S(2)}, u32[]{:S(2)}) collective-permute-start(bf16[8,128,1024]{2,1,0:T(8,128)(2,1)} %bitcast.11), channel_id=1, source_target_pairs={{1,0},{0,1},{3,2},{2,3},{5,4},{4,5},{7,6},{6,7},{9,8},{8,9},{11,10... | collective-permute-start | bytes 6291464 | tf_op jit(solution)/shard_map/ppermute | solution.py:348
  0.7 26.6 %collective-permute-start.2 = (s32[2,6]{1,0:T(2,128)S(1)}, s32[2,6]{1,0:T(2,128)S(1)}, u32[]{:S(2)}, u32[]{:S(2)}) collective-permute-start(s32[2,6]{1,0:T(2,128)S(1)} %compare_select_fusion), channel_id=1, source_target_pairs={{0,2},{1,3},{2,4},{3,5},{4,6},{5,7},{6,8},{7,9},{8,10},{9,11},{10,... | collective-permute-start | bytes 152 | tf_op jit(solution)/shard_map/ppermute | solution.py:345
  2.3 24.9 %collective-permute-start.1 = (s32[2,6]{1,0:T(2,128)S(1)}, s32[2,6]{1,0:T(2,128)S(1)}, u32[]{:S(2)}, u32[]{:S(2)}) collective-permute-start(s32[2,6]{1,0:T(2,128)S(1)} %compare_select_fusion), channel_id=1, source_target_pairs={{0,126},{1,127},{2,0},{3,1},{4,2},{5,3},{6,4},{7,5},{8,6},{9,7},{1... | collective-permute-start | bytes 152 | tf_op jit(solution)/shard_map/ppermute | solution.py:345
  28.0 17.5 %collective-permute-start.3 = (bf16[2,128,1024]{2,1,0:T(8,128)(2,1)S(1)}, bf16[2,128,1024]{2,1,0:T(8,128)(2,1)S(1)}, u32[]{:S(2)}, u32[]{:S(2)}) collective-permute-start(bf16[2,128,1024]{2,1,0:T(8,128)(2,1)S(1)} %get-tuple-element.18), channel_id=1, source_target_pairs={{126,0},{127,1},{0,2},{1,3},{2,4},{3,5},{4,6},{5,7},{6,8},{7,9},{8... | collective-permute-start | bytes 1572872 | tf_op jit(solution)/shard_map/ppermute | solution.py:348
  28.1 6.3 %copy-start = (s32[2,6]{1,0:T(2,128)S(1)}, s32[2,6]{1,0:T(2,128)}, u32[]{:S(2)}) copy-start(s32[2,6]{1,0:T(2,128)} %tiles_ref.5) | copy-start | bytes 148
  28.1 6.3 %copy-start.1 = (s32[2,6]{1,0:T(2,128)S(1)}, s32[2,6]{1,0:T(2,128)}, u32[]{:S(2)}) copy-start(s32[2,6]{1,0:T(2,128)} %live_ref.5) | copy-start | bytes 148
  28.1 6.3 %copy-start.2 = (bf16[1024,2048]{1,0:T(8,128)(2,1)S(1)}, bf16[1024,2048]{1,0:T(8,128)(2,1)}, u32[]{:S(2)}) copy-start(bf16[1024,2048]{1,0:T(8,128)(2,1)} %w_keyval.5) | copy-start | bytes 12582916
  28.1 6.3 %copy-start.3 = (bf16[1024,1024]{1,0:T(8,128)(2,1)S(1)}, bf16[1024,1024]{1,0:T(8,128)(2,1)}, u32[]{:S(2)}) copy-start(bf16[1024,1024]{1,0:T(8,128)(2,1)} %w_query.1) | copy-start | bytes 6291460
  28.2 6.3 %copy-start.5 = (bf16[256,1024]{1,0:T(8,128)(2,1)S(1)}, bf16[256,1024]{1,0:T(8,128)(2,1)}, u32[]{:S(2)}) copy-start(bf16[256,1024]{1,0:T(8,128)(2,1)} %mesh.3) | copy-start | bytes 1572868
  28.2 17.7 %collective-permute-start.4 = (bf16[2,128,1024]{2,1,0:T(8,128)(2,1)S(1)}, bf16[2,128,1024]{2,1,0:T(8,128)(2,1)S(1)}, u32[]{:S(2)}, u32[]{:S(2)}) collective-permute-start(bf16[2,128,1024]{2,1,0:T(8,128)(2,1)S(1)} %get-tuple-element.19), channel_id=1, source_target_pairs={{2,0},{3,1},{4,2},{5,3},{6,4},{7,5},{8,6},{9,7},{10,8},{11,9},{12,... | collective-permute-start | bytes 1572872 | tf_op jit(solution)/shard_map/ppermute | solution.py:348
  34.2 16.8 %collective-permute-start.5 = (bf16[2,128,1024]{2,1,0:T(8,128)(2,1)S(1)}, bf16[2,128,1024]{2,1,0:T(8,128)(2,1)S(1)}, u32[]{:S(2)}, u32[]{:S(2)}) collective-permute-start(bf16[2,128,1024]{2,1,0:T(8,128)(2,1)S(1)} %shard_map.74), channel_id=1, source_target_pairs={{126,0},{3,1},{0,2},{5,3},{2,4},{7,5},{4,6},{9,7},{6,8},{11,9},{8,... | collective-permute-start | bytes 1572872 | tf_op jit(solution)/shard_map/ppermute | solution.py:348
  45.9 5.2 %copy-start.4 = (bf16[1024,1024]{1,0:T(8,128)(2,1)S(1)}, bf16[1024,1024]{1,0:T(8,128)(2,1)}, u32[]{:S(2)}) copy-start(bf16[1024,1024]{1,0:T(8,128)(2,1)} %w_out.1) | copy-start | bytes 6291460

commit v4 on v3

--- a/solution.py
+++ b/solution.py
@@ -41,7 +41,7 @@
 
 
 SOURCES = (behind_of, ahead_of, cross_of)
-STAGES = ((0, 1),)
+STAGES = (0, 1)
 LAST = 2
 
 
@@ -271,47 +271,39 @@
     lax.fori_loop(0, (count + group - 1) // group, body, 0)
 
 
-def chunk_update(sources, own, tiles_ref, live_ref, rows_ref, w_keyval, keys, values, *state):
+def chunk_update(source, own, tiles_ref, live_ref, rows, w_keyval, keys, values, *state):
     me = lax.axis_index("nodes")
     n = lax.axis_size("nodes")
     listed = [
         jnp.where(live > 0, tile, -1)
         for tile, live in zip(entries(tiles_ref), entries(live_ref))
     ]
-    project(rows_ref, w_keyval, keys, values, w_keyval.shape[0])
-    wanted = []
-    for source in sources:
-        base = source(me, n) * own
-        low, high = span_of(listed, base, own)
-        wanted.append(jnp.where(low < own, base + low, -1))
-        wanted.append(jnp.where(low < high, base + high, -1))
+    base = source(me, n) * own
+    low, high = span_of(listed, base, own)
+    wanted = (base + low, jnp.where(low < high, base + high, -1))
 
     def keep(tile):
-        found = wanted[0]
-        for k in range(1, len(wanted)):
-            found = jnp.where(tile == k, wanted[k], found)
+        found = jnp.where(tile == 0, wanted[0], wanted[1])
         return found, found >= 0
 
-    add_listed(len(wanted), keep, tiles_ref, live_ref, keys, values, *state)
-
-
-def chunk_kernel(sources, own, tiles_ref, live_ref, w_keyval, queries, tops_in, totals_in, mixed_in, *refs):
-    count = len(sources)
-    chunks, (tops, totals, mixed, rows, keys, values) = refs[:count], refs[count:]
+    @pl.when(high >= 0)
+    def _():
+        project(rows, w_keyval, keys, values, w_keyval.shape[0])
+        add_listed(CAP, keep, tiles_ref, live_ref, keys, values, *state)
+
+
+def chunk_kernel(source, own, tiles_ref, live_ref, w_keyval, queries, tops_in, totals_in, mixed_in, chunk, tops, totals, mixed, keys, values):
     tops[...] = tops_in[...]
     totals[...] = totals_in[...]
     mixed[...] = mixed_in[...]
-    for k, chunk in enumerate(chunks):
-        size = chunk.shape[0]
-        rows[k * size : (k + 1) * size, :] = chunk[...]
-    chunk_update(sources, own, tiles_ref, live_ref, rows, w_keyval, keys, values, queries, tops, totals, mixed)
-
-
-def last_kernel(sources, own, tiles_ref, live_ref, w_keyval, queries, tops_in, totals_in, mixed_in, chunk, mesh, w_out, out, tops, totals, mixed, keys, values):
+    chunk_update(source, own, tiles_ref, live_ref, chunk, w_keyval, keys, values, queries, tops, totals, mixed)
+
+
+def last_kernel(source, own, tiles_ref, live_ref, w_keyval, queries, tops_in, totals_in, mixed_in, chunk, mesh, w_out, out, tops, totals, mixed, keys, values):
     tops[...] = tops_in[...]
     totals[...] = totals_in[...]
     mixed[...] = mixed_in[...]
-    chunk_update(sources, own, tiles_ref, live_ref, chunk, w_keyval, keys, values, queries, tops, totals, mixed)
+    chunk_update(source, own, tiles_ref, live_ref, chunk, w_keyval, keys, values, queries, tops, totals, mixed)
     pairs = queries.shape[1]
     width = queries.shape[2]
     head = width // 2
@@ -399,26 +391,23 @@
         w_query,
     )
 
-    for members in STAGES:
-        sources = [SOURCES[c] for c in members]
-        rows = len(members) * CAP * TILE
+    for stage in STAGES:
         tops, totals, mixed = pl.pallas_call(
-            functools.partial(chunk_kernel, sources, own),
+            functools.partial(chunk_kernel, SOURCES[stage], own),
             out_shape=[stat, stat, mix],
-            in_specs=[SMEM, SMEM] + [VMEM] * (5 + len(members)),
+            in_specs=[SMEM, SMEM] + [VMEM] * 6,
             out_specs=[VMEM] * 3,
             scratch_shapes=[
-                pltpu.VMEM((rows, model_width), bf16),
-                pltpu.VMEM((rows, model_width), bf16),
-                pltpu.VMEM((rows // TILE, model_width, TILE), bf16),
+                pltpu.VMEM((CAP * TILE, model_width), bf16),
+                pltpu.VMEM((CAP, model_width, TILE), bf16),
             ],
             input_output_aliases={4: 0, 5: 1, 6: 2},
             compiler_params=pltpu.CompilerParams(vmem_limit_bytes=12 * MIB),
             cost_estimate=pl.CostEstimate(flops=2 * 10**9, transcendentals=0, bytes_accessed=10**6),
             name="chunk",
-        )(neighbour_tiles, neighbour_live, w_keyval, queries, tops, totals, mixed, *[chunks[c] for c in members])
+        )(neighbour_tiles, neighbour_live, w_keyval, queries, tops, totals, mixed, chunks[stage])
     return pl.pallas_call(
-        functools.partial(last_kernel, [SOURCES[LAST]], own),
+        functools.partial(last_kernel, SOURCES[LAST], own),
         out_shape=jax.ShapeDtypeStruct(mesh_latents.shape, f32),
         in_specs=[SMEM, SMEM] + [VMEM] * 8,
         out_specs=VMEM,

time: 55.7 us -> 55.7 us (level)
    pallas_call x2 -> x3, Pallas kernels: 9.59 us -> 9.23 us  [the longest x2 4.74 us: per_device(): pl.pallas_call(functools.partial(chunk_kernel, SOURCES[stage], own), out_...]
  transfers between devices with their start and end apart: 6 -> 6, of which waited for: 2 -> 2; matrix products, arithmetic and copies ran while one was open for 1% -> 1% of each run, Pallas kernels for 33% -> 32%
where the time goes in v4:
time: 55.7 us; the launch traced here: 55.6 us
  starting transfers between devices  30.7 us (55%)
  Pallas kernels  22.1 us (40%)
  waiting for transfers between devices  1.91 us (3%)
  other arithmetic  0.7 us (1%)
    ppermute x2, starting transfers between devices, to_sources(): return lax.ppermute(block, 'nodes', [(i, source(i, n)) for i in range(n)])  25 us
    pallas_call x1, Pallas kernels, per_device(): pl.pallas_call(own_kernel, out_shape=[query, stat, stat, mix], in_specs=[...  9.95 us
    ppermute x4, starting transfers between devices, from_sources(): return lax.ppermute(block, 'nodes', [(source(i, n), i) for i in range(n)])  5.68 us
    pallas_call x2, Pallas kernels, per_device(): pl.pallas_call(functools.partial(chunk_kernel, SOURCES[stage], own), out_...  4.74 us
    pallas_call x1, Pallas kernels, per_device(): pl.pallas_call(functools.partial(last_kernel, SOURCES[LAST], own), out_sh...  4.49 us
    ppermute x4, waiting for transfers between devices, from_sources(): return lax.ppermute(block, 'nodes', [(source(i, n), i) for i in range(n)])  1.9 us
    pallas_call x1, Pallas kernels, per_device(): pl.pallas_call(front_kernel, out_shape=jax.ShapeDtypeStruct(tiled.shape,...  1.56 us
    pallas_call x2, Pallas kernels, pack(): pl.pallas_call(kernel, out_shape=[shape] * count, in_specs=[SMEM, SMEM, V...  1.34 us
  transfers between devices with their start and end apart: 6, of which 2 were waited for; matrix products, arithmetic and copies ran while one was open for 1% of the time, Pallas kernels for 32%

profile of v4, /device:TPU:40, one launch (start us, length us, event | category | flops | bytes accessed | tf_op | source)
XLA Modules:
  0.0 55.6 jit_solution(16399066993597175696)
XLA Ops:
  0.0 0.0 collective-permute-start
  0.0 0.7 %compare_select_fusion = s32[2,6]{1,0:T(2,128)S(1)} fusion(s32[2,6]{1,0:T(2,128)} %tiles_ref.7, s32[2,6]{1,0:T(2,128)} %live_ref.7), kind=kLoop, calls=%fused_computation | loop fusion | flops 24 | bytes 144 | tf_op jit(solution)/shard_map/jit(_where)/select_n | solution.py:348
  0.7 1.6 %collective-permute-start.2 = (s32[2,6]{1,0:T(2,128)S(1)}, s32[2,6]{1,0:T(2,128)S(1)}, u32[]{:S(2)}, u32[]{:S(2)}) collective-permute-start(s32[2,6]{1,0:T(2,128)S(1)} %compare_select_fusion), channel_id=1, source_target_pairs={{0,2},{1,3},{2,4},{3,5},{4,6},{5,7},{6,8},{7,9},{8,10},{9,11},{10,... | collective-permute-start | bytes 152 | tf_op jit(solution)/shard_map/ppermute | solution.py:337
  2.3 23.4 %collective-permute-start.1 = (s32[2,6]{1,0:T(2,128)S(1)}, s32[2,6]{1,0:T(2,128)S(1)}, u32[]{:S(2)}, u32[]{:S(2)}) collective-permute-start(s32[2,6]{1,0:T(2,128)S(1)} %compare_select_fusion), channel_id=1, source_target_pairs={{0,126},{1,127},{2,0},{3,1},{4,2},{5,3},{6,4},{7,5},{8,6},{9,7},{1... | collective-permute-start | bytes 152 | tf_op jit(solution)/shard_map/ppermute | solution.py:337
  25.7 1.6 %front.1.grid = bf16[8,128,1024]{2,1,0:T(8,128)(2,1)S(1)} custom-call(bf16[8,128,1024]{2,1,0:T(8,128)(2,1)} %bitcast.12), custom_call_target="tpu_custom_call" | custom-call | flops 100000000 | bytes 1000000 | tf_op jit(solution)/shard_map/front/pallas_call | solution.py:355
  27.3 0.0 collective-permute-done.2.from_behind
  27.3 0.0 collective-permute-done.1.from_ahead
  27.3 0.7 %shard_map.73 = (bf16[2,128,1024]{2,1,0:T(8,128)(2,1)S(1)}, bf16[2,128,1024]{2,1,0:T(8,128)(2,1)S(1)}) custom-call(s32[2,6]{1,0:T(2,128)S(1)} %collective-permute-done.1.from_ahead, s32[2,6]{1,0:T(2,128)S(1)} %collective-permute-done.2.from_behind, bf16[8,128,1024]{2,1,0:T(8,128)(2,1)S(1)} %front.1.grid), custom_call_target="tpu_custom_call" | custom-call | flops 2000000000 | bytes 1000000 | tf_op jit(solution)/shard_map/pallas_call | solution.py:89
  28.0 0.1 collective-permute-start.3
  28.1 0.0 copy-start
  28.1 0.0 copy-start.1
  28.1 0.0 copy-start.2
  28.1 0.0 copy-start.3
  28.2 0.0 copy-start.5
  28.2 5.4 %collective-permute-start.4 = (bf16[2,128,1024]{2,1,0:T(8,128)(2,1)S(1)}, bf16[2,128,1024]{2,1,0:T(8,128)(2,1)S(1)}, u32[]{:S(2)}, u32[]{:S(2)}) collective-permute-start(bf16[2,128,1024]{2,1,0:T(8,128)(2,1)S(1)} %get-tuple-element.25), channel_id=1, source_target_pairs={{2,0},{3,1},{4,2},{5,3},{6,4},{7,5},{8,6},{9,7},{10,8},{11,9},{12,... | collective-permute-start | bytes 1572872 | tf_op jit(solution)/shard_map/ppermute | solution.py:340
  33.6 0.6 %shard_map.74 = bf16[2,128,1024]{2,1,0:T(8,128)(2,1)S(1)} custom-call(s32[2,6]{1,0:T(2,128)S(1)} %collective-permute-done.1.from_ahead, s32[2,6]{1,0:T(2,128)S(1)} %collective-permute-done.2.from_behind, bf16[8,128,1024]{2,1,0:T(8,128)(2,1)S(1)} %collective-permute-done.grid), custom_call_target="tpu_custom_call" | custom-call | flops 2000000000 | bytes 1000000 | tf_op jit(solution)/shard_map/pallas_call | solution.py:89
  34.2 0.1 collective-permute-start.5
  34.4 10.0 %own.1 = (bf16[2,8,128,256]{3,2,1,0:T(8,128)(2,1)S(1)}, f32[2,8,256]{2,1,0:T(8,128)S(1)}, f32[2,8,256]{2,1,0:T(8,128)S(1)}, f32[2,1024,128]{2,1,0:T(8,128)S(1)}) custom-call(s32[2,6]{1,0:T(2,128)S(1)} %copy-done, s32[2,6]{1,0:T(2,128)S(1)} %copy-done.1, bf16[1024,1024]{1,0:T(8,128)(2,1)S(1)} %bitcast.6, bf16[1024,1024]{1,0:T(8,128)(2,1)S(1)} %bitcast.7, ...), custom_call_target="tpu_custom_call" | custom-call | flops 6000000000 | bytes 10000000 | tf_op jit(solution)/shard_map/own/pallas_call | solution.py:370
  44.4 1.1 %collective-permute-done.3 = bf16[2,128,1024]{2,1,0:T(8,128)(2,1)S(1)} collective-permute-done((bf16[2,128,1024]{2,1,0:T(8,128)(2,1)S(1)}, bf16[2,128,1024]{2,1,0:T(8,128)(2,1)S(1)}, u32[]{:S(2)}, u32[]{:S(2)}) %collective-permute-start.3) | collective-permute-done | bytes 524320 | tf_op jit(solution)/shard_map/ppermute | solution.py:340
  45.5 4.0 %chunk.2 = (f32[2,8,256]{2,1,0:T(8,128)S(1)}, f32[2,8,256]{2,1,0:T(8,128)S(1)}, f32[2,1024,128]{2,1,0:T(8,128)S(1)}) custom-call(s32[2,6]{1,0:T(2,128)S(1)} %copy-done, s32[2,6]{1,0:T(2,128)S(1)} %copy-done.1, bf16[1024,2048]{1,0:T(8,128)(2,1)S(1)} %copy-done.2, ...), custom_call_target="tpu_custom_call", output_to_operand_aliasing={{0}: (4, {}), {1}: (5, {}), {2}: (6, {})} | custom-call | flops 2000000000 | bytes 1000000 | tf_op jit(solution)/shard_map/chunk/pallas_call | solution.py:395
  49.5 0.0 copy-start.4
  49.5 0.7 %chunk.3 = (f32[2,8,256]{2,1,0:T(8,128)S(1)}, f32[2,8,256]{2,1,0:T(8,128)S(1)}, f32[2,1024,128]{2,1,0:T(8,128)S(1)}) custom-call(s32[2,6]{1,0:T(2,128)S(1)} %copy-done, s32[2,6]{1,0:T(2,128)S(1)} %copy-done.1, bf16[1024,2048]{1,0:T(8,128)(2,1)S(1)} %copy-done.2, ...), custom_call_target="tpu_custom_call", output_to_operand_aliasing={{0}: (4, {}), {1}: (5, {}), {2}: (6, {})} | custom-call | flops 2000000000 | bytes 1000000 | tf_op jit(solution)/shard_map/chunk/pallas_call | solution.py:395
  50.2 0.8 %collective-permute-done.5 = bf16[2,128,1024]{2,1,0:T(8,128)(2,1)S(1)} collective-permute-done((bf16[2,128,1024]{2,1,0:T(8,128)(2,1)S(1)}, bf16[2,128,1024]{2,1,0:T(8,128)(2,1)S(1)}, u32[]{:S(2)}, u32[]{:S(2)}) %collective-permute-start.5) | collective-permute-done | bytes 524320 | tf_op jit(solution)/shard_map/ppermute | solution.py:340
  51.1 4.5 %last.1 = f32[256,1024]{1,0:T(8,128)} custom-call(s32[2,6]{1,0:T(2,128)S(1)} %copy-done, s32[2,6]{1,0:T(2,128)S(1)} %copy-done.1, bf16[1024,2048]{1,0:T(8,128)(2,1)S(1)} %copy-done.2, bf16[2,8,128,256]{3,2,1,0:T(8,128)(2,1)S(1)} %get-tuple-element.17.queries, f32[2,8,256]{2,1,0:T(8,128)S(1)} %get-tuple-element.26.tops_in, ...), custom_call_target="tpu_custom_call" | custom-call | flops 3000000000 | bytes 1000000 | tf_op jit(solution)/shard_map/last/pallas_call | solution.py:409
  (8 shorter events, 0.0 us)
Async XLA Ops:
  0.0 33.6 %collective-permute-start = (bf16[8,128,1024]{2,1,0:T(8,128)(2,1)}, bf16[8,128,1024]{2,1,0:T(8,128)(2,1)S(1)}, u32[]{:S(2)}, u32[]{:S(2)}) collective-permute-start(bf16[8,128,1024]{2,1,0:T(8,128)(2,1)} %bitcast.11), channel_id=1, source_target_pairs={{1,0},{0,1},{3,2},{2,3},{5,4},{4,5},{7,6},{6,7},{9,8},{8,9},{11,10... | collective-permute-start | bytes 6291464 | tf_op jit(solution)/shard_map/ppermute | solution.py:340
  0.7 26.6 %collective-permute-start.2 = (s32[2,6]{1,0:T(2,128)S(1)}, s32[2,6]{1,0:T(2,128)S(1)}, u32[]{:S(2)}, u32[]{:S(2)}) collective-permute-start(s32[2,6]{1,0:T(2,128)S(1)} %compare_select_fusion), channel_id=1, source_target_pairs={{0,2},{1,3},{2,4},{3,5},{4,6},{5,7},{6,8},{7,9},{8,10},{9,11},{10,... | collective-permute-start | bytes 152 | tf_op jit(solution)/shard_map/ppermute | solution.py:337
  2.3 24.9 %collective-permute-start.1 = (s32[2,6]{1,0:T(2,128)S(1)}, s32[2,6]{1,0:T(2,128)S(1)}, u32[]{:S(2)}, u32[]{:S(2)}) collective-permute-start(s32[2,6]{1,0:T(2,128)S(1)} %compare_select_fusion), channel_id=1, source_target_pairs={{0,126},{1,127},{2,0},{3,1},{4,2},{5,3},{6,4},{7,5},{8,6},{9,7},{1... | collective-permute-start | bytes 152 | tf_op jit(solution)/shard_map/ppermute | solution.py:337
  28.0 17.5 %collective-permute-start.3 = (bf16[2,128,1024]{2,1,0:T(8,128)(2,1)S(1)}, bf16[2,128,1024]{2,1,0:T(8,128)(2,1)S(1)}, u32[]{:S(2)}, u32[]{:S(2)}) collective-permute-start(bf16[2,128,1024]{2,1,0:T(8,128)(2,1)S(1)} %get-tuple-element.21), channel_id=1, source_target_pairs={{126,0},{127,1},{0,2},{1,3},{2,4},{3,5},{4,6},{5,7},{6,8},{7,9},{8... | collective-permute-start | bytes 1572872 | tf_op jit(solution)/shard_map/ppermute | solution.py:340
  28.1 6.3 %copy-start = (s32[2,6]{1,0:T(2,128)S(1)}, s32[2,6]{1,0:T(2,128)}, u32[]{:S(2)}) copy-start(s32[2,6]{1,0:T(2,128)} %tiles_ref.7) | copy-start | bytes 148
  28.1 6.3 %copy-start.1 = (s32[2,6]{1,0:T(2,128)S(1)}, s32[2,6]{1,0:T(2,128)}, u32[]{:S(2)}) copy-start(s32[2,6]{1,0:T(2,128)} %live_ref.7) | copy-start | bytes 148
  28.1 6.3 %copy-start.2 = (bf16[1024,2048]{1,0:T(8,128)(2,1)S(1)}, bf16[1024,2048]{1,0:T(8,128)(2,1)}, u32[]{:S(2)}) copy-start(bf16[1024,2048]{1,0:T(8,128)(2,1)} %w_keyval.7) | copy-start | bytes 12582916
  28.1 6.3 %copy-start.3 = (bf16[1024,1024]{1,0:T(8,128)(2,1)S(1)}, bf16[1024,1024]{1,0:T(8,128)(2,1)}, u32[]{:S(2)}) copy-start(bf16[1024,1024]{1,0:T(8,128)(2,1)} %w_query.1) | copy-start | bytes 6291460
  28.2 6.3 %copy-start.5 = (bf16[256,1024]{1,0:T(8,128)(2,1)S(1)}, bf16[256,1024]{1,0:T(8,128)(2,1)}, u32[]{:S(2)}) copy-start(bf16[256,1024]{1,0:T(8,128)(2,1)} %mesh.3) | copy-start | bytes 1572868
  28.2 21.3 %collective-permute-start.4 = (bf16[2,128,1024]{2,1,0:T(8,128)(2,1)S(1)}, bf16[2,128,1024]{2,1,0:T(8,128)(2,1)S(1)}, u32[]{:S(2)}, u32[]{:S(2)}) collective-permute-start(bf16[2,128,1024]{2,1,0:T(8,128)(2,1)S(1)} %get-tuple-element.25), channel_id=1, source_target_pairs={{2,0},{3,1},{4,2},{5,3},{6,4},{7,5},{8,6},{9,7},{10,8},{11,9},{12,... | collective-permute-start | bytes 1572872 | tf_op jit(solution)/shard_map/ppermute | solution.py:340
  34.2 16.8 %collective-permute-start.5 = (bf16[2,128,1024]{2,1,0:T(8,128)(2,1)S(1)}, bf16[2,128,1024]{2,1,0:T(8,128)(2,1)S(1)}, u32[]{:S(2)}, u32[]{:S(2)}) collective-permute-start(bf16[2,128,1024]{2,1,0:T(8,128)(2,1)S(1)} %shard_map.74), channel_id=1, source_target_pairs={{126,0},{3,1},{0,2},{5,3},{2,4},{7,5},{4,6},{9,7},{6,8},{11,9},{8,... | collective-permute-start | bytes 1572872 | tf_op jit(solution)/shard_map/ppermute | solution.py:340
  49.5 1.6 %copy-start.4 = (bf16[1024,1024]{1,0:T(8,128)(2,1)S(1)}, bf16[1024,1024]{1,0:T(8,128)(2,1)}, u32[]{:S(2)}) copy-start(bf16[1024,1024]{1,0:T(8,128)(2,1)} %w_out.1) | copy-start | bytes 6291460

commit v5 on v4

--- a/solution.py
+++ b/solution.py
@@ -187,7 +187,7 @@
         copy.wait()
 
 
-def form_queries(mesh, w_query, queries):
+def query_kernel(mesh, w_query, queries):
     model_width = w_query.shape[0]
     head = queries.shape[2] // 2
     step = 256
@@ -206,10 +206,9 @@
                 ]
 
 
-def own_kernel(tiles_ref, live_ref, grid, beside, w_keyval, mesh, w_query, queries, tops, totals, mixed, rows, keys, values, found):
+def own_kernel(tiles_ref, live_ref, grid, beside, w_keyval, queries, tops, totals, mixed, rows, keys, values, found):
     own = grid.shape[0] // TILE
     mesh_tiles = tiles_ref.shape[0]
-    form_queries(mesh, w_query, queries)
     tops[...] = jnp.full(tops.shape, LOW, jnp.float32)
     totals[...] = jnp.zeros(totals.shape, jnp.float32)
     mixed[...] = jnp.zeros(mixed.shape, jnp.float32)
@@ -271,7 +270,11 @@
     lax.fori_loop(0, (count + group - 1) // group, body, 0)
 
 
-def chunk_update(source, own, tiles_ref, live_ref, rows, w_keyval, keys, values, *state):
+def chunk_update(source, own, tiles_ref, live_ref, rows, w_keyval, keys, values, queries, before, after):
+    def carry_state():
+        for old, new in zip(before, after):
+            new[...] = old[...]
+
     me = lax.axis_index("nodes")
     n = lax.axis_size("nodes")
     listed = [
@@ -289,21 +292,20 @@
     @pl.when(high >= 0)
     def _():
         project(rows, w_keyval, keys, values, w_keyval.shape[0])
-        add_listed(CAP, keep, tiles_ref, live_ref, keys, values, *state)
+        carry_state()
+        add_listed(CAP, keep, tiles_ref, live_ref, keys, values, queries, *after)
+
+    @pl.when(high < 0)
+    def _():
+        carry_state()
 
 
 def chunk_kernel(source, own, tiles_ref, live_ref, w_keyval, queries, tops_in, totals_in, mixed_in, chunk, tops, totals, mixed, keys, values):
-    tops[...] = tops_in[...]
-    totals[...] = totals_in[...]
-    mixed[...] = mixed_in[...]
-    chunk_update(source, own, tiles_ref, live_ref, chunk, w_keyval, keys, values, queries, tops, totals, mixed)
+    chunk_update(source, own, tiles_ref, live_ref, chunk, w_keyval, keys, values, queries, (tops_in, totals_in, mixed_in), (tops, totals, mixed))
 
 
 def last_kernel(source, own, tiles_ref, live_ref, w_keyval, queries, tops_in, totals_in, mixed_in, chunk, mesh, w_out, out, tops, totals, mixed, keys, values):
-    tops[...] = tops_in[...]
-    totals[...] = totals_in[...]
-    mixed[...] = mixed_in[...]
-    chunk_update(source, own, tiles_ref, live_ref, chunk, w_keyval, keys, values, queries, tops, totals, mixed)
+    chunk_update(source, own, tiles_ref, live_ref, chunk, w_keyval, keys, values, queries, (tops_in, totals_in, mixed_in), (tops, totals, mixed))
     pairs = queries.shape[1]
     width = queries.shape[2]
     head = width // 2
@@ -359,19 +361,28 @@
         out_specs=VMEM,
         scratch_shapes=[pltpu.SemaphoreType.DMA((2,))],
         compiler_params=pltpu.CompilerParams(vmem_limit_bytes=4 * MIB),
-        cost_estimate=pl.CostEstimate(flops=10**8, transcendentals=0, bytes_accessed=10**6),
+        cost_estimate=pl.CostEstimate(flops=2 * 10**9, transcendentals=0, bytes_accessed=10**6),
         name="front",
     )(stored)
+    queries = pl.pallas_call(
+        query_kernel,
+        out_shape=query,
+        in_specs=[VMEM] * 2,
+        out_specs=VMEM,
+        compiler_params=pltpu.CompilerParams(vmem_limit_bytes=8 * MIB),
+        cost_estimate=pl.CostEstimate(flops=10**9, transcendentals=0, bytes_accessed=10**6),
+        name="query",
+    )(mesh_latents, w_query)
     packed = pack(pack_kernel, 2, asked, near)
     packed += pack(relay_kernel, 1, asked, beside)
     chunks = []
     for block, source in zip(packed, (behind_of, ahead_of, relay_of)):
         chunks.append(from_sources(block, source).reshape(CAP * TILE, model_width))
-    queries, tops, totals, mixed = pl.pallas_call(
+    tops, totals, mixed = pl.pallas_call(
         own_kernel,
-        out_shape=[query, stat, stat, mix],
-        in_specs=[SMEM, SMEM] + [VMEM] * 5,
-        out_specs=[VMEM] * 4,
+        out_shape=[stat, stat, mix],
+        in_specs=[SMEM, SMEM] + [VMEM] * 4,
+        out_specs=[VMEM] * 3,
         scratch_shapes=[
             pltpu.VMEM((CAP * TILE, model_width), bf16),
             pltpu.VMEM((CAP * TILE, model_width), bf16),
@@ -387,8 +398,7 @@
         near.reshape(own * TILE, model_width),
         beside.reshape(own * TILE, model_width),
         w_keyval,
-        mesh_latents,
-        w_query,
+        queries,
     )
 
     for stage in STAGES:

time: 55.7 us -> 59.2 us (1.063)
  local copies, waits for them, and re-layouts: 0.04 us -> 2.66 us
  waiting for transfers between devices: 1.91 us -> 2.92 us
    unnamed x12 -> x14, local copies, waits for them, and re-layouts: 0.04 us -> 2.66 us
    ppermute x4, waiting for transfers between devices: 1.9 us -> 2.91 us  [from_sources(): return lax.ppermute(block, 'nodes', [(source(i, n), i) for i in range(n)])]
    pallas_call x1 -> x2, Pallas kernels: 9.95 us -> 9.94 us  [the longest x1 9.16 us: per_device(): pl.pallas_call(own_kernel, out_shape=[stat, stat, mix], in_specs=[SMEM, S...]
  transfers between devices with their start and end apart: 6 -> 6, of which waited for: 2 -> 2; matrix products, arithmetic and copies ran while one was open for 1% -> 1% of each run, Pallas kernels for 32% -> 30%
where the time goes in v5:
time: 59.2 us; the launch traced here: 58.9 us
  starting transfers between devices  30.5 us (52%)
  Pallas kernels  21.9 us (37%)
  waiting for transfers between devices  2.92 us (5%)
  local copies, waits for them, and re-layouts  2.66 us (4%)
  other arithmetic  0.7 us (1%)
    ppermute x2, starting transfers between devices, to_sources(): return lax.ppermute(block, 'nodes', [(i, source(i, n)) for i in range(n)])  25 us
    pallas_call x1, Pallas kernels, per_device(): pl.pallas_call(own_kernel, out_shape=[stat, stat, mix], in_specs=[SMEM, S...  9.16 us
    ppermute x4, starting transfers between devices, from_sources(): return lax.ppermute(block, 'nodes', [(source(i, n), i) for i in range(n)])  5.56 us
    pallas_call x2, Pallas kernels, per_device(): pl.pallas_call(functools.partial(chunk_kernel, SOURCES[stage], own), out_...  4.68 us
    pallas_call x1, Pallas kernels, per_device(): pl.pallas_call(functools.partial(last_kernel, SOURCES[LAST], own), out_sh...  4.42 us
    ppermute x4, waiting for transfers between devices, from_sources(): return lax.ppermute(block, 'nodes', [(source(i, n), i) for i in range(n)])  2.91 us
    unnamed x14, local copies, waits for them, and re-layouts  2.66 us
    pallas_call x1, Pallas kernels, per_device(): pl.pallas_call(front_kernel, out_shape=jax.ShapeDtypeStruct(tiled.shape,...  1.56 us
  transfers between devices with their start and end apart: 6, of which 2 were waited for; matrix products, arithmetic and copies ran while one was open for 1% of the time, Pallas kernels for 30%

profile of v5, /device:TPU:40, one launch (start us, length us, event | category | flops | bytes accessed | tf_op | source)
XLA Modules:
  0.0 58.9 jit_solution(16474883404808612216)
XLA Ops:
  0.0 0.0 collective-permute-start
  0.0 0.7 %compare_select_fusion = s32[2,6]{1,0:T(2,128)S(1)} fusion(s32[2,6]{1,0:T(2,128)} %tiles_ref.7, s32[2,6]{1,0:T(2,128)} %live_ref.7), kind=kLoop, calls=%fused_computation | loop fusion | flops 24 | bytes 144 | tf_op jit(solution)/shard_map/jit(_where)/select_n | solution.py:350
  0.7 1.6 %collective-permute-start.2 = (s32[2,6]{1,0:T(2,128)S(1)}, s32[2,6]{1,0:T(2,128)S(1)}, u32[]{:S(2)}, u32[]{:S(2)}) collective-permute-start(s32[2,6]{1,0:T(2,128)S(1)} %compare_select_fusion), channel_id=1, source_target_pairs={{0,2},{1,3},{2,4},{3,5},{4,6},{5,7},{6,8},{7,9},{8,10},{9,11},{10,... | collective-permute-start | bytes 152 | tf_op jit(solution)/shard_map/ppermute | solution.py:339
  2.3 23.4 %collective-permute-start.1 = (s32[2,6]{1,0:T(2,128)S(1)}, s32[2,6]{1,0:T(2,128)S(1)}, u32[]{:S(2)}, u32[]{:S(2)}) collective-permute-start(s32[2,6]{1,0:T(2,128)S(1)} %compare_select_fusion), channel_id=1, source_target_pairs={{0,126},{1,127},{2,0},{3,1},{4,2},{5,3},{6,4},{7,5},{8,6},{9,7},{1... | collective-permute-start | bytes 152 | tf_op jit(solution)/shard_map/ppermute | solution.py:339
  25.7 1.6 %copy-done.3 = bf16[1024,1024]{1,0:T(8,128)(2,1)S(1)} copy-done((bf16[1024,1024]{1,0:T(8,128)(2,1)S(1)}, bf16[1024,1024]{1,0:T(8,128)(2,1)}, u32[]{:S(2)}) %copy-start.3) | copy-done | bytes 2097176
  27.3 1.0 %copy-done.5 = bf16[256,1024]{1,0:T(8,128)(2,1)S(1)} copy-done((bf16[256,1024]{1,0:T(8,128)(2,1)S(1)}, bf16[256,1024]{1,0:T(8,128)(2,1)}, u32[]{:S(2)}) %copy-start.5) | copy-done | bytes 524312
  28.3 0.8 %query.1.queries = bf16[2,8,128,256]{3,2,1,0:T(8,128)(2,1)S(1)} custom-call(bf16[256,1024]{1,0:T(8,128)(2,1)S(1)} %copy-done.5, bf16[1024,1024]{1,0:T(8,128)(2,1)S(1)} %copy-done.3), custom_call_target="tpu_custom_call" | custom-call | flops 1000000000 | bytes 1000000 | tf_op jit(solution)/shard_map/query/pallas_call | solution.py:367
  29.1 1.6 %front.1.grid = bf16[8,128,1024]{2,1,0:T(8,128)(2,1)S(1)} custom-call(bf16[8,128,1024]{2,1,0:T(8,128)(2,1)} %bitcast.12), custom_call_target="tpu_custom_call" | custom-call | flops 2000000000 | bytes 1000000 | tf_op jit(solution)/shard_map/front/pallas_call | solution.py:357
  30.7 0.7 %shard_map.73 = (bf16[2,128,1024]{2,1,0:T(8,128)(2,1)S(1)}, bf16[2,128,1024]{2,1,0:T(8,128)(2,1)S(1)}) custom-call(s32[2,6]{1,0:T(2,128)S(1)} %collective-permute-done.1.from_ahead, s32[2,6]{1,0:T(2,128)S(1)} %collective-permute-done.2.from_behind, bf16[8,128,1024]{2,1,0:T(8,128)(2,1)S(1)} %front.1.grid), custom_call_target="tpu_custom_call" | custom-call | flops 2000000000 | bytes 1000000 | tf_op jit(solution)/shard_map/pallas_call | solution.py:89
  31.4 0.1 collective-permute-start.3
  31.5 0.0 copy-start
  31.5 0.0 copy-start.1
  31.6 0.0 copy-start.2
  31.6 5.3 %collective-permute-start.4 = (bf16[2,128,1024]{2,1,0:T(8,128)(2,1)S(1)}, bf16[2,128,1024]{2,1,0:T(8,128)(2,1)S(1)}, u32[]{:S(2)}, u32[]{:S(2)}) collective-permute-start(bf16[2,128,1024]{2,1,0:T(8,128)(2,1)S(1)} %get-tuple-element.23), channel_id=1, source_target_pairs={{2,0},{3,1},{4,2},{5,3},{6,4},{7,5},{8,6},{9,7},{10,8},{11,9},{12,... | collective-permute-start | bytes 1572872 | tf_op jit(solution)/shard_map/ppermute | solution.py:342
  36.9 0.6 %shard_map.74 = bf16[2,128,1024]{2,1,0:T(8,128)(2,1)S(1)} custom-call(s32[2,6]{1,0:T(2,128)S(1)} %collective-permute-done.1.from_ahead, s32[2,6]{1,0:T(2,128)S(1)} %collective-permute-done.2.from_behind, bf16[8,128,1024]{2,1,0:T(8,128)(2,1)S(1)} %collective-permute-done.grid), custom_call_target="tpu_custom_call" | custom-call | flops 2000000000 | bytes 1000000 | tf_op jit(solution)/shard_map/pallas_call | solution.py:89
  37.5 0.1 collective-permute-start.5
  37.7 9.2 %own.1 = (f32[2,8,256]{2,1,0:T(8,128)S(1)}, f32[2,8,256]{2,1,0:T(8,128)S(1)}, f32[2,1024,128]{2,1,0:T(8,128)S(1)}) custom-call(s32[2,6]{1,0:T(2,128)S(1)} %copy-done, s32[2,6]{1,0:T(2,128)S(1)} %copy-done.1, bf16[1024,1024]{1,0:T(8,128)(2,1)S(1)} %bitcast.10, bf16[1024,1024]{1,0:T(8,128)(2,1)S(1)} %bitcast.6, bf16[1024,2048]{1,0:T(8,128)(2,1)S(1)} %copy-done.2, ...), custom_call_target="tpu_custom_call" | custom-call | flops 6000000000 | bytes 10000000 | tf_op jit(solution)/shard_map/own/pallas_call | solution.py:381
  46.9 2.0 %collective-permute-done.3 = bf16[2,128,1024]{2,1,0:T(8,128)(2,1)S(1)} collective-permute-done((bf16[2,128,1024]{2,1,0:T(8,128)(2,1)S(1)}, bf16[2,128,1024]{2,1,0:T(8,128)(2,1)S(1)}, u32[]{:S(2)}, u32[]{:S(2)}) %collective-permute-start.3) | collective-permute-done | bytes 524320 | tf_op jit(solution)/shard_map/ppermute | solution.py:342
  48.9 3.9 %chunk.2 = (f32[2,8,256]{2,1,0:T(8,128)S(1)}, f32[2,8,256]{2,1,0:T(8,128)S(1)}, f32[2,1024,128]{2,1,0:T(8,128)S(1)}) custom-call(s32[2,6]{1,0:T(2,128)S(1)} %copy-done, s32[2,6]{1,0:T(2,128)S(1)} %copy-done.1, bf16[1024,2048]{1,0:T(8,128)(2,1)S(1)} %copy-done.2, ...), custom_call_target="tpu_custom_call", output_to_operand_aliasing={{0}: (4, {}), {1}: (5, {}), {2}: (6, {})} | custom-call | flops 2000000000 | bytes 1000000 | tf_op jit(solution)/shard_map/chunk/pallas_call | solution.py:405
  52.8 0.0 copy-start.4
  52.8 0.0 copy-start.6
  52.8 0.8 %chunk.3 = (f32[2,8,256]{2,1,0:T(8,128)S(1)}, f32[2,8,256]{2,1,0:T(8,128)S(1)}, f32[2,1024,128]{2,1,0:T(8,128)S(1)}) custom-call(s32[2,6]{1,0:T(2,128)S(1)} %copy-done, s32[2,6]{1,0:T(2,128)S(1)} %copy-done.1, bf16[1024,2048]{1,0:T(8,128)(2,1)S(1)} %copy-done.2, ...), custom_call_target="tpu_custom_call", output_to_operand_aliasing={{0}: (4, {}), {1}: (5, {}), {2}: (6, {})} | custom-call | flops 2000000000 | bytes 1000000 | tf_op jit(solution)/shard_map/chunk/pallas_call | solution.py:405
  53.6 0.9 %collective-permute-done.5 = bf16[2,128,1024]{2,1,0:T(8,128)(2,1)S(1)} collective-permute-done((bf16[2,128,1024]{2,1,0:T(8,128)(2,1)S(1)}, bf16[2,128,1024]{2,1,0:T(8,128)(2,1)S(1)}, u32[]{:S(2)}, u32[]{:S(2)}) %collective-permute-start.5) | collective-permute-done | bytes 524320 | tf_op jit(solution)/shard_map/ppermute | solution.py:342
  54.5 4.4 %last.1 = f32[256,1024]{1,0:T(8,128)} custom-call(s32[2,6]{1,0:T(2,128)S(1)} %copy-done, s32[2,6]{1,0:T(2,128)S(1)} %copy-done.1, bf16[1024,2048]{1,0:T(8,128)(2,1)S(1)} %copy-done.2, bf16[2,8,128,256]{3,2,1,0:T(8,128)(2,1)S(1)} %query.1.queries, f32[2,8,256]{2,1,0:T(8,128)S(1)} %get-tuple-element.24.tops_in, f32[2,8,256]{2,1,0:T(8,128)S(1)} %get-tuple-element.25.totals_in, ...), custom_call_target="tpu_custom_call" | custom-call | flops 3000000000 | bytes 1000000 | tf_op jit(solution)/shard_map/last/pallas_call | solution.py:419
  (11 shorter events, 0.0 us)
Async XLA Ops:
  0.0 36.9 %collective-permute-start = (bf16[8,128,1024]{2,1,0:T(8,128)(2,1)}, bf16[8,128,1024]{2,1,0:T(8,128)(2,1)S(1)}, u32[]{:S(2)}, u32[]{:S(2)}) collective-permute-start(bf16[8,128,1024]{2,1,0:T(8,128)(2,1)} %bitcast.11), channel_id=1, source_target_pairs={{1,0},{0,1},{3,2},{2,3},{5,4},{4,5},{7,6},{6,7},{9,8},{8,9},{11,10... | collective-permute-start | bytes 6291464 | tf_op jit(solution)/shard_map/ppermute | solution.py:342
  0.7 30.0 %collective-permute-start.2 = (s32[2,6]{1,0:T(2,128)S(1)}, s32[2,6]{1,0:T(2,128)S(1)}, u32[]{:S(2)}, u32[]{:S(2)}) collective-permute-start(s32[2,6]{1,0:T(2,128)S(1)} %compare_select_fusion), channel_id=1, source_target_pairs={{0,2},{1,3},{2,4},{3,5},{4,6},{5,7},{6,8},{7,9},{8,10},{9,11},{10,... | collective-permute-start | bytes 152 | tf_op jit(solution)/shard_map/ppermute | solution.py:339
  2.3 28.4 %collective-permute-start.1 = (s32[2,6]{1,0:T(2,128)S(1)}, s32[2,6]{1,0:T(2,128)S(1)}, u32[]{:S(2)}, u32[]{:S(2)}) collective-permute-start(s32[2,6]{1,0:T(2,128)S(1)} %compare_select_fusion), channel_id=1, source_target_pairs={{0,126},{1,127},{2,0},{3,1},{4,2},{5,3},{6,4},{7,5},{8,6},{9,7},{1... | collective-permute-start | bytes 152 | tf_op jit(solution)/shard_map/ppermute | solution.py:339
  25.7 1.6 %copy-start.3 = (bf16[1024,1024]{1,0:T(8,128)(2,1)S(1)}, bf16[1024,1024]{1,0:T(8,128)(2,1)}, u32[]{:S(2)}) copy-start(bf16[1024,1024]{1,0:T(8,128)(2,1)} %w_query.1) | copy-start | bytes 6291460
  27.3 1.0 %copy-start.5 = (bf16[256,1024]{1,0:T(8,128)(2,1)S(1)}, bf16[256,1024]{1,0:T(8,128)(2,1)}, u32[]{:S(2)}) copy-start(bf16[256,1024]{1,0:T(8,128)(2,1)} %mesh.3) | copy-start | bytes 1572868
  31.4 17.5 %collective-permute-start.3 = (bf16[2,128,1024]{2,1,0:T(8,128)(2,1)S(1)}, bf16[2,128,1024]{2,1,0:T(8,128)(2,1)S(1)}, u32[]{:S(2)}, u32[]{:S(2)}) collective-permute-start(bf16[2,128,1024]{2,1,0:T(8,128)(2,1)S(1)} %get-tuple-element.19), channel_id=1, source_target_pairs={{126,0},{127,1},{0,2},{1,3},{2,4},{3,5},{4,6},{5,7},{6,8},{7,9},{8... | collective-permute-start | bytes 1572872 | tf_op jit(solution)/shard_map/ppermute | solution.py:342
  31.5 6.1 %copy-start = (s32[2,6]{1,0:T(2,128)S(1)}, s32[2,6]{1,0:T(2,128)}, u32[]{:S(2)}) copy-start(s32[2,6]{1,0:T(2,128)} %tiles_ref.7) | copy-start | bytes 148
  31.5 6.1 %copy-start.1 = (s32[2,6]{1,0:T(2,128)S(1)}, s32[2,6]{1,0:T(2,128)}, u32[]{:S(2)}) copy-start(s32[2,6]{1,0:T(2,128)} %live_ref.7) | copy-start | bytes 148
  31.6 6.1 %copy-start.2 = (bf16[1024,2048]{1,0:T(8,128)(2,1)S(1)}, bf16[1024,2048]{1,0:T(8,128)(2,1)}, u32[]{:S(2)}) copy-start(bf16[1024,2048]{1,0:T(8,128)(2,1)} %w_keyval.7) | copy-start | bytes 12582916
  31.6 21.2 %collective-permute-start.4 = (bf16[2,128,1024]{2,1,0:T(8,128)(2,1)S(1)}, bf16[2,128,1024]{2,1,0:T(8,128)(2,1)S(1)}, u32[]{:S(2)}, u32[]{:S(2)}) collective-permute-start(bf16[2,128,1024]{2,1,0:T(8,128)(2,1)S(1)} %get-tuple-element.23), channel_id=1, source_target_pairs={{2,0},{3,1},{4,2},{5,3},{6,4},{7,5},{8,6},{9,7},{10,8},{11,9},{12,... | collective-permute-start | bytes 1572872 | tf_op jit(solution)/shard_map/ppermute | solution.py:342
  37.5 17.0 %collective-permute-start.5 = (bf16[2,128,1024]{2,1,0:T(8,128)(2,1)S(1)}, bf16[2,128,1024]{2,1,0:T(8,128)(2,1)S(1)}, u32[]{:S(2)}, u32[]{:S(2)}) collective-permute-start(bf16[2,128,1024]{2,1,0:T(8,128)(2,1)S(1)} %shard_map.74), channel_id=1, source_target_pairs={{126,0},{3,1},{0,2},{5,3},{2,4},{7,5},{4,6},{9,7},{6,8},{11,9},{8,... | collective-permute-start | bytes 1572872 | tf_op jit(solution)/shard_map/ppermute | solution.py:342
  52.8 1.7 %copy-start.4 = (bf16[1024,1024]{1,0:T(8,128)(2,1)S(1)}, bf16[1024,1024]{1,0:T(8,128)(2,1)}, u32[]{:S(2)}) copy-start(bf16[1024,1024]{1,0:T(8,128)(2,1)} %w_out.1) | copy-start | bytes 6291460
  52.8 1.7 %copy-start.6 = (bf16[256,1024]{1,0:T(8,128)(2,1)S(1)}, bf16[256,1024]{1,0:T(8,128)(2,1)}, u32[]{:S(2)}) copy-start(bf16[256,1024]{1,0:T(8,128)(2,1)} %mesh.3) | copy-start | bytes 1572868

commit v6 on v5

--- a/solution.py
+++ b/solution.py
@@ -119,34 +119,50 @@
                 ]
 
 
-def add_tile(tile, mesh_tile, keys, values, queries, tops, totals, mixed):
+def add_tiles(tiles, mesh_tile, keys, values, queries, tops, totals, mixed):
     pairs = queries.shape[1]
     width = queries.shape[2]
     head = width // 2
-    start = pl.multiple_of(tile * TILE, TILE)
+    starts = [pl.multiple_of(tile * TILE, TILE) for tile in tiles]
     for pair in range(pairs):
         lanes = slice(pair * width, (pair + 1) * width)
-        scores = jnp.dot(
-            keys[pl.ds(start, TILE), lanes],
-            queries[mesh_tile, pair],
-            preferred_element_type=jnp.float32,
-        )
+        scores = [
+            jnp.dot(
+                keys[pl.ds(start, TILE), lanes],
+                queries[mesh_tile, pair],
+                preferred_element_type=jnp.float32,
+            )
+            for start in starts
+        ]
         old = tops[mesh_tile, pair : pair + 1, :]
-        new = jnp.maximum(old, jnp.max(scores, axis=0, keepdims=True))
+        highest = functools.reduce(jnp.maximum, scores)
+        new = jnp.maximum(old, jnp.max(highest, axis=0, keepdims=True))
         shrink = jnp.exp(old - new)
-        raised = jnp.exp(scores - new)
+        raised = [jnp.exp(part - new) for part in scores]
         tops[mesh_tile, pair : pair + 1, :] = new
         totals[mesh_tile, pair : pair + 1, :] = totals[
             mesh_tile, pair : pair + 1, :
-        ] * shrink + jnp.sum(raised, axis=0, keepdims=True)
-        weights = raised.astype(jnp.bfloat16)
+        ] * shrink + jnp.sum(functools.reduce(jnp.add, raised), axis=0, keepdims=True)
+        weights = jnp.concatenate([part.astype(jnp.bfloat16) for part in raised], axis=0)
         for k in range(2):
             rows = slice(pair * width + k * head, pair * width + (k + 1) * head)
             cols = slice(k * TILE, (k + 1) * TILE)
             part = jnp.dot(
-                values[tile, rows, :], weights[:, cols], preferred_element_type=jnp.float32
+                jnp.concatenate([values[tile, rows, :] for tile in tiles], axis=1),
+                weights[:, cols],
+                preferred_element_type=jnp.float32,
             )
             mixed[mesh_tile, rows, :] = mixed[mesh_tile, rows, :] * shrink[:, cols] + part
+
+
+def add_pair(first, second, mesh_tile, *state):
+    @pl.when(first & second)
+    def _():
+        add_tiles((0, 1), mesh_tile, *state)
+
+    @pl.when(first != second)
+    def _():
+        add_tiles((jnp.where(first, 0, 1),), mesh_tile, *state)
 
 
 def lists(tiles_ref, live_ref, mesh_tile, wanted):
@@ -156,21 +172,15 @@
     return found
 
 
-def add_listed(count, keep, tiles_ref, live_ref, *state):
-    mesh_tiles = tiles_ref.shape[0]
-
-    def body(i, carry):
-        tile = i // mesh_tiles
-        mesh_tile = i % mesh_tiles
-        wanted, fresh = keep(tile)
-
-        @pl.when(fresh & lists(tiles_ref, live_ref, mesh_tile, wanted))
-        def _():
-            add_tile(tile, mesh_tile, *state)
-
+def add_listed(wanted, tiles_ref, live_ref, *state):
+    def body(mesh_tile, carry):
+        first, second = (
+            (tile >= 0) & lists(tiles_ref, live_ref, mesh_tile, tile) for tile in wanted
+        )
+        add_pair(first, second, mesh_tile, *state)
         return carry
 
-    lax.fori_loop(0, count * mesh_tiles, body, 0)
+    lax.fori_loop(0, tiles_ref.shape[0], body, 0)
 
 
 def front_kernel(grid_hbm, grid, sems):
@@ -228,10 +238,13 @@
             mask = mask | jnp.where(taken, lax.shift_left(jnp.int32(1), jnp.maximum(bit, 0)), 0)
         masks.append(mask)
     union = functools.reduce(jnp.bitwise_or, masks)
+    shared = functools.reduce(jnp.bitwise_and, masks)
+    leading = masks[0] & ~shared
     count = jnp.int32(0)
-    for bit in range(2 * own):
-        found[count] = jnp.int32(bit)
-        count = count + ((union >> bit) & 1)
+    for members in (leading, shared, union & ~shared & ~leading):
+        for bit in range(2 * own):
+            found[count] = jnp.int32(bit)
+            count = count + ((members >> bit) & 1)
     found[count] = jnp.int32(0)
     group = rows.shape[0] // TILE
 
@@ -250,22 +263,18 @@
 
         project(rows, w_keyval, keys, values, w_keyval.shape[0])
 
-        def visit(i, inner):
-            k = i // mesh_tiles
-            m = i % mesh_tiles
-            place = g * group + k
+        def visit(m, inner):
             mask = masks[0]
             for other in range(1, mesh_tiles):
                 mask = jnp.where(m == other, masks[other], mask)
-            taken = (lax.shift_right_logical(mask, found[place]) & 1) > 0
-
-            @pl.when(taken & (place < count))
-            def _():
-                add_tile(k, m, keys, values, queries, tops, totals, mixed)
-
+            first, second = (
+                ((lax.shift_right_logical(mask, found[place]) & 1) > 0) & (place < count)
+                for place in (g * group, g * group + 1)
+            )
+            add_pair(first, second, m, keys, values, queries, tops, totals, mixed)
             return inner
 
-        return lax.fori_loop(0, group * mesh_tiles, visit, carry)
+        return lax.fori_loop(0, mesh_tiles, visit, carry)
 
     lax.fori_loop(0, (count + group - 1) // group, body, 0)
 
@@ -285,15 +294,11 @@
     low, high = span_of(listed, base, own)
     wanted = (base + low, jnp.where(low < high, base + high, -1))
 
-    def keep(tile):
-        found = jnp.where(tile == 0, wanted[0], wanted[1])
-        return found, found >= 0
-
     @pl.when(high >= 0)
     def _():
         project(rows, w_keyval, keys, values, w_keyval.shape[0])
         carry_state()
-        add_listed(CAP, keep, tiles_ref, live_ref, keys, values, queries, *after)
+        add_listed(wanted, tiles_ref, live_ref, keys, values, queries, *after)
 
     @pl.when(high < 0)
     def _():
@@ -361,7 +366,7 @@
         out_specs=VMEM,
         scratch_shapes=[pltpu.SemaphoreType.DMA((2,))],
         compiler_params=pltpu.CompilerParams(vmem_limit_bytes=4 * MIB),
-        cost_estimate=pl.CostEstimate(flops=2 * 10**9, transcendentals=0, bytes_accessed=10**6),
+        cost_estimate=pl.CostEstimate(flops=10**8, transcendentals=0, bytes_accessed=10**6),
         name="front",
     )(stored)
     queries = pl.pallas_call(
@@ -387,7 +392,7 @@
             pltpu.VMEM((CAP * TILE, model_width), bf16),
             pltpu.VMEM((CAP * TILE, model_width), bf16),
             pltpu.VMEM((CAP, model_width, TILE), bf16),
-            pltpu.SMEM((2 * own + 1,), jnp.int32),
+            pltpu.SMEM((2 * own + 2,), jnp.int32),
         ],
         compiler_params=pltpu.CompilerParams(vmem_limit_bytes=12 * MIB),
         cost_estimate=pl.CostEstimate(flops=6 * 10**9, transcendentals=0, bytes_accessed=10**7),

time: 59.2 us -> 58 us (0.980)
  Pallas kernels: 21.9 us -> 25.6 us
  waiting for transfers between devices: 2.92 us -> 0.02 us
  local copies, waits for them, and re-layouts: 2.66 us -> 0.65 us
    ppermute x4, waiting for transfers between devices: 2.91 us -> 0.01 us  [from_sources(): return lax.ppermute(block, 'nodes', [(source(i, n), i) for i in range(n)])]
    pallas_call x1, Pallas kernels: 9.16 us -> 11.8 us  [per_device(): pl.pallas_call(own_kernel, out_shape=[stat, stat, mix], in_specs=[SMEM, S...]
    unnamed x14 -> x12, local copies, waits for them, and re-layouts: 2.66 us -> 0.65 us
    pallas_call x2, Pallas kernels: 4.68 us -> 5.73 us  [per_device(): pl.pallas_call(functools.partial(chunk_kernel, SOURCES[stage], own), out_...]
  transfers between devices with their start and end apart: 6 -> 6, of which waited for: 2 -> 0; matrix products, arithmetic and copies ran while one was open for 1% -> 1% of each run, Pallas kernels for 30% -> 37%
where the time goes in v6:
time: 58 us; the launch traced here: 57.8 us
  starting transfers between devices  30.7 us (53%)
  Pallas kernels  25.6 us (44%)
  other arithmetic  0.7 us (1%)
  local copies, waits for them, and re-layouts  0.65 us (1%)
    ppermute x2, starting transfers between devices, to_sources(): return lax.ppermute(block, 'nodes', [(i, source(i, n)) for i in range(n)])  25.1 us
    pallas_call x1, Pallas kernels, per_device(): pl.pallas_call(own_kernel, out_shape=[stat, stat, mix], in_specs=[SMEM, S...  11.8 us
    pallas_call x2, Pallas kernels, per_device(): pl.pallas_call(functools.partial(chunk_kernel, SOURCES[stage], own), out_...  5.73 us
    ppermute x4, starting transfers between devices, from_sources(): return lax.ppermute(block, 'nodes', [(source(i, n), i) for i in range(n)])  5.56 us
    pallas_call x1, Pallas kernels, per_device(): pl.pallas_call(functools.partial(last_kernel, SOURCES[LAST], own), out_sh...  4.34 us
    pallas_call x1, Pallas kernels, per_device(): pl.pallas_call(front_kernel, out_shape=jax.ShapeDtypeStruct(tiled.shape,...  1.56 us
    pallas_call x2, Pallas kernels, pack(): pl.pallas_call(kernel, out_shape=[shape] * count, in_specs=[SMEM, SMEM, V...  1.34 us
  transfers between devices with their start and end apart: 6, of which 0 were waited for; matrix products, arithmetic and copies ran while one was open for 1% of the time, Pallas kernels for 37%

profile of v6, /device:TPU:40, one launch (start us, length us, event | category | flops | bytes accessed | tf_op | source)
XLA Modules:
  0.0 57.8 jit_solution(8778683501412141128)
XLA Ops:
  0.0 0.0 collective-permute-start
  0.0 0.7 %compare_select_fusion = s32[2,6]{1,0:T(2,128)S(1)} fusion(s32[2,6]{1,0:T(2,128)} %tiles_ref.7, s32[2,6]{1,0:T(2,128)} %live_ref.7), kind=kLoop, calls=%fused_computation | loop fusion | flops 24 | bytes 144 | tf_op jit(solution)/shard_map/jit(_where)/select_n | solution.py:355
  0.7 1.6 %collective-permute-start.2 = (s32[2,6]{1,0:T(2,128)S(1)}, s32[2,6]{1,0:T(2,128)S(1)}, u32[]{:S(2)}, u32[]{:S(2)}) collective-permute-start(s32[2,6]{1,0:T(2,128)S(1)} %compare_select_fusion), channel_id=1, source_target_pairs={{0,2},{1,3},{2,4},{3,5},{4,6},{5,7},{6,8},{7,9},{8,10},{9,11},{10,... | collective-permute-start | bytes 152 | tf_op jit(solution)/shard_map/ppermute | solution.py:344
  2.3 23.5 %collective-permute-start.1 = (s32[2,6]{1,0:T(2,128)S(1)}, s32[2,6]{1,0:T(2,128)S(1)}, u32[]{:S(2)}, u32[]{:S(2)}) collective-permute-start(s32[2,6]{1,0:T(2,128)S(1)} %compare_select_fusion), channel_id=1, source_target_pairs={{0,126},{1,127},{2,0},{3,1},{4,2},{5,3},{6,4},{7,5},{8,6},{9,7},{1... | collective-permute-start | bytes 152 | tf_op jit(solution)/shard_map/ppermute | solution.py:344
  25.8 1.6 %front.1.grid = bf16[8,128,1024]{2,1,0:T(8,128)(2,1)S(1)} custom-call(bf16[8,128,1024]{2,1,0:T(8,128)(2,1)} %bitcast.12), custom_call_target="tpu_custom_call" | custom-call | flops 100000000 | bytes 1000000 | tf_op jit(solution)/shard_map/front/pallas_call | solution.py:362
  27.4 0.8 %query.1.queries = bf16[2,8,128,256]{3,2,1,0:T(8,128)(2,1)S(1)} custom-call(bf16[256,1024]{1,0:T(8,128)(2,1)S(1)} %copy-done.5, bf16[1024,1024]{1,0:T(8,128)(2,1)S(1)} %copy-done.3), custom_call_target="tpu_custom_call" | custom-call | flops 1000000000 | bytes 1000000 | tf_op jit(solution)/shard_map/query/pallas_call | solution.py:372
  28.2 0.0 collective-permute-done.2.from_behind
  28.2 0.0 collective-permute-done.1.from_ahead
  28.2 0.7 %shard_map.73 = (bf16[2,128,1024]{2,1,0:T(8,128)(2,1)S(1)}, bf16[2,128,1024]{2,1,0:T(8,128)(2,1)S(1)}) custom-call(s32[2,6]{1,0:T(2,128)S(1)} %collective-permute-done.1.from_ahead, s32[2,6]{1,0:T(2,128)S(1)} %collective-permute-done.2.from_behind, bf16[8,128,1024]{2,1,0:T(8,128)(2,1)S(1)} %front.1.grid), custom_call_target="tpu_custom_call" | custom-call | flops 2000000000 | bytes 1000000 | tf_op jit(solution)/shard_map/pallas_call | solution.py:89
  28.9 0.1 collective-permute-start.3
  29.1 0.0 copy-start
  29.1 0.0 copy-start.1
  29.1 0.0 copy-start.2
  29.1 5.3 %collective-permute-start.4 = (bf16[2,128,1024]{2,1,0:T(8,128)(2,1)S(1)}, bf16[2,128,1024]{2,1,0:T(8,128)(2,1)S(1)}, u32[]{:S(2)}, u32[]{:S(2)}) collective-permute-start(bf16[2,128,1024]{2,1,0:T(8,128)(2,1)S(1)} %get-tuple-element.23), channel_id=1, source_target_pairs={{2,0},{3,1},{4,2},{5,3},{6,4},{7,5},{8,6},{9,7},{10,8},{11,9},{12,... | collective-permute-start | bytes 1572872 | tf_op jit(solution)/shard_map/ppermute | solution.py:347
  34.4 0.0 collective-permute-done.grid
  34.4 0.6 %shard_map.74 = bf16[2,128,1024]{2,1,0:T(8,128)(2,1)S(1)} custom-call(s32[2,6]{1,0:T(2,128)S(1)} %collective-permute-done.1.from_ahead, s32[2,6]{1,0:T(2,128)S(1)} %collective-permute-done.2.from_behind, bf16[8,128,1024]{2,1,0:T(8,128)(2,1)S(1)} %collective-permute-done.grid), custom_call_target="tpu_custom_call" | custom-call | flops 2000000000 | bytes 1000000 | tf_op jit(solution)/shard_map/pallas_call | solution.py:89
  35.0 0.1 collective-permute-start.5
  35.2 11.8 %own.1 = (f32[2,8,256]{2,1,0:T(8,128)S(1)}, f32[2,8,256]{2,1,0:T(8,128)S(1)}, f32[2,1024,128]{2,1,0:T(8,128)S(1)}) custom-call(s32[2,6]{1,0:T(2,128)S(1)} %copy-done, s32[2,6]{1,0:T(2,128)S(1)} %copy-done.1, bf16[1024,1024]{1,0:T(8,128)(2,1)S(1)} %bitcast.6, bf16[1024,1024]{1,0:T(8,128)(2,1)S(1)} %bitcast.7, bf16[1024,2048]{1,0:T(8,128)(2,1)S(1)} %copy-done.2, ...), custom_call_target="tpu_custom_call" | custom-call | flops 6000000000 | bytes 10000000 | tf_op jit(solution)/shard_map/own/pallas_call | solution.py:386
  47.1 0.0 collective-permute-done.3
  47.1 4.8 %chunk.2 = (f32[2,8,256]{2,1,0:T(8,128)S(1)}, f32[2,8,256]{2,1,0:T(8,128)S(1)}, f32[2,1024,128]{2,1,0:T(8,128)S(1)}) custom-call(s32[2,6]{1,0:T(2,128)S(1)} %copy-done, s32[2,6]{1,0:T(2,128)S(1)} %copy-done.1, bf16[1024,2048]{1,0:T(8,128)(2,1)S(1)} %copy-done.2, ...), custom_call_target="tpu_custom_call", output_to_operand_aliasing={{0}: (4, {}), {1}: (5, {}), {2}: (6, {})} | custom-call | flops 2000000000 | bytes 1000000 | tf_op jit(solution)/shard_map/chunk/pallas_call | solution.py:410
  51.9 0.0 copy-start.4
  51.9 0.9 %chunk.3 = (f32[2,8,256]{2,1,0:T(8,128)S(1)}, f32[2,8,256]{2,1,0:T(8,128)S(1)}, f32[2,1024,128]{2,1,0:T(8,128)S(1)}) custom-call(s32[2,6]{1,0:T(2,128)S(1)} %copy-done, s32[2,6]{1,0:T(2,128)S(1)} %copy-done.1, bf16[1024,2048]{1,0:T(8,128)(2,1)S(1)} %copy-done.2, ...), custom_call_target="tpu_custom_call", output_to_operand_aliasing={{0}: (4, {}), {1}: (5, {}), {2}: (6, {})} | custom-call | flops 2000000000 | bytes 1000000 | tf_op jit(solution)/shard_map/chunk/pallas_call | solution.py:410
  52.9 0.6 %copy-done.4 = bf16[1024,1024]{1,0:T(8,128)(2,1)S(1)} copy-done((bf16[1024,1024]{1,0:T(8,128)(2,1)S(1)}, bf16[1024,1024]{1,0:T(8,128)(2,1)}, u32[]{:S(2)}) %copy-start.4) | copy-done | bytes 2097176
  53.5 4.3 %last.1 = f32[256,1024]{1,0:T(8,128)} custom-call(s32[2,6]{1,0:T(2,128)S(1)} %copy-done, s32[2,6]{1,0:T(2,128)S(1)} %copy-done.1, bf16[1024,2048]{1,0:T(8,128)(2,1)S(1)} %copy-done.2, bf16[2,8,128,256]{3,2,1,0:T(8,128)(2,1)S(1)} %query.1.queries, f32[2,8,256]{2,1,0:T(8,128)S(1)} %get-tuple-element.24.tops_in, f32[2,8,256]{2,1,0:T(8,128)S(1)} %get-tuple-element.25.totals_in, ...), custom_call_target="tpu_custom_call" | custom-call | flops 3000000000 | bytes 1000000 | tf_op jit(solution)/shard_map/last/pallas_call | solution.py:424
  (9 shorter events, 0.0 us)
Async XLA Ops:
  0.0 34.4 %collective-permute-start = (bf16[8,128,1024]{2,1,0:T(8,128)(2,1)}, bf16[8,128,1024]{2,1,0:T(8,128)(2,1)S(1)}, u32[]{:S(2)}, u32[]{:S(2)}) collective-permute-start(bf16[8,128,1024]{2,1,0:T(8,128)(2,1)} %bitcast.11), channel_id=1, source_target_pairs={{1,0},{0,1},{3,2},{2,3},{5,4},{4,5},{7,6},{6,7},{9,8},{8,9},{11,10... | collective-permute-start | bytes 6291464 | tf_op jit(solution)/shard_map/ppermute | solution.py:347
  0.7 26.7 %copy-start.3 = (bf16[1024,1024]{1,0:T(8,128)(2,1)S(1)}, bf16[1024,1024]{1,0:T(8,128)(2,1)}, u32[]{:S(2)}) copy-start(bf16[1024,1024]{1,0:T(8,128)(2,1)} %w_query.1) | copy-start | bytes 6291460
  0.7 26.7 %copy-start.5 = (bf16[256,1024]{1,0:T(8,128)(2,1)S(1)}, bf16[256,1024]{1,0:T(8,128)(2,1)}, u32[]{:S(2)}) copy-start(bf16[256,1024]{1,0:T(8,128)(2,1)} %mesh.3) | copy-start | bytes 1572868
  0.7 27.5 %collective-permute-start.2 = (s32[2,6]{1,0:T(2,128)S(1)}, s32[2,6]{1,0:T(2,128)S(1)}, u32[]{:S(2)}, u32[]{:S(2)}) collective-permute-start(s32[2,6]{1,0:T(2,128)S(1)} %compare_select_fusion), channel_id=1, source_target_pairs={{0,2},{1,3},{2,4},{3,5},{4,6},{5,7},{6,8},{7,9},{8,10},{9,11},{10,... | collective-permute-start | bytes 152 | tf_op jit(solution)/shard_map/ppermute | solution.py:344
  2.3 25.9 %collective-permute-start.1 = (s32[2,6]{1,0:T(2,128)S(1)}, s32[2,6]{1,0:T(2,128)S(1)}, u32[]{:S(2)}, u32[]{:S(2)}) collective-permute-start(s32[2,6]{1,0:T(2,128)S(1)} %compare_select_fusion), channel_id=1, source_target_pairs={{0,126},{1,127},{2,0},{3,1},{4,2},{5,3},{6,4},{7,5},{8,6},{9,7},{1... | collective-permute-start | bytes 152 | tf_op jit(solution)/shard_map/ppermute | solution.py:344
  28.9 18.2 %collective-permute-start.3 = (bf16[2,128,1024]{2,1,0:T(8,128)(2,1)S(1)}, bf16[2,128,1024]{2,1,0:T(8,128)(2,1)S(1)}, u32[]{:S(2)}, u32[]{:S(2)}) collective-permute-start(bf16[2,128,1024]{2,1,0:T(8,128)(2,1)S(1)} %get-tuple-element.19), channel_id=1, source_target_pairs={{126,0},{127,1},{0,2},{1,3},{2,4},{3,5},{4,6},{5,7},{6,8},{7,9},{8... | collective-permute-start | bytes 1572872 | tf_op jit(solution)/shard_map/ppermute | solution.py:347
  29.1 6.1 %copy-start = (s32[2,6]{1,0:T(2,128)S(1)}, s32[2,6]{1,0:T(2,128)}, u32[]{:S(2)}) copy-start(s32[2,6]{1,0:T(2,128)} %tiles_ref.7) | copy-start | bytes 148
  29.1 6.1 %copy-start.1 = (s32[2,6]{1,0:T(2,128)S(1)}, s32[2,6]{1,0:T(2,128)}, u32[]{:S(2)}) copy-start(s32[2,6]{1,0:T(2,128)} %live_ref.7) | copy-start | bytes 148
  29.1 6.1 %copy-start.2 = (bf16[1024,2048]{1,0:T(8,128)(2,1)S(1)}, bf16[1024,2048]{1,0:T(8,128)(2,1)}, u32[]{:S(2)}) copy-start(bf16[1024,2048]{1,0:T(8,128)(2,1)} %w_keyval.7) | copy-start | bytes 12582916
  29.1 22.8 %collective-permute-start.4 = (bf16[2,128,1024]{2,1,0:T(8,128)(2,1)S(1)}, bf16[2,128,1024]{2,1,0:T(8,128)(2,1)S(1)}, u32[]{:S(2)}, u32[]{:S(2)}) collective-permute-start(bf16[2,128,1024]{2,1,0:T(8,128)(2,1)S(1)} %get-tuple-element.23), channel_id=1, source_target_pairs={{2,0},{3,1},{4,2},{5,3},{6,4},{7,5},{8,6},{9,7},{10,8},{11,9},{12,... | collective-permute-start | bytes 1572872 | tf_op jit(solution)/shard_map/ppermute | solution.py:347
  35.0 17.8 %collective-permute-start.5 = (bf16[2,128,1024]{2,1,0:T(8,128)(2,1)S(1)}, bf16[2,128,1024]{2,1,0:T(8,128)(2,1)S(1)}, u32[]{:S(2)}, u32[]{:S(2)}) collective-permute-start(bf16[2,128,1024]{2,1,0:T(8,128)(2,1)S(1)} %shard_map.74), channel_id=1, source_target_pairs={{126,0},{3,1},{0,2},{5,3},{2,4},{7,5},{4,6},{9,7},{6,8},{11,9},{8,... | collective-permute-start | bytes 1572872 | tf_op jit(solution)/shard_map/ppermute | solution.py:347
  51.9 1.6 %copy-start.4 = (bf16[1024,1024]{1,0:T(8,128)(2,1)S(1)}, bf16[1024,1024]{1,0:T(8,128)(2,1)}, u32[]{:S(2)}) copy-start(bf16[1024,1024]{1,0:T(8,128)(2,1)} %w_out.1) | copy-start | bytes 6291460
